TPU v7x, 512 devices: a 4x2x32 block of a 4x8x32 slice. The times are simulated.
512 devices in a mesh: groups: 2 (over y), sample: 32 (over z), fsdp: 4 (over x), prompt: 2 (over core).
Axes of the slice: x: 4, y: 2, z: 32, core: 2. Of those that a mesh axis runs over, the one named last changes fastest.
The devices are a block of a 4x8x32 slice.
Arguments:
- queries: bfloat16 [4, 32, 512, 4096], P(('groups', 'prompt'), 'sample', 'fsdp'), parts along dimension 0, may hold values from -16 to 16
- completion_keys: bfloat16 [4, 32, 512, 512], P(('groups', 'prompt'), 'sample', 'fsdp'), parts along dimension 0, may hold values from -6 to 6
- completion_values: bfloat16 [4, 32, 512, 512], P(('groups', 'prompt'), 'sample', 'fsdp'), parts along dimension 0, may hold values from -6 to 6
- prompt_keys: bfloat16 [4, 128, 512], P(('groups', 'prompt'), ('sample', 'fsdp')), parts along dimension 0, may hold values from -6 to 6
- prompt_values: bfloat16 [4, 128, 512], P(('groups', 'prompt'), ('sample', 'fsdp')), parts along dimension 0, may hold values from -6 to 6
- output_grad: bfloat16 [4, 32, 512, 4096], P(('groups', 'prompt'), 'sample', 'fsdp'), parts along dimension 0, may hold values from -6 to 6
- lengths: int32 [4, 32], P(('groups', 'prompt'), 'sample'), parts along dimension 0, may hold values from 128 to 512
Outputs:
- attention_out: bfloat16 [4, 32, 512, 4096], P(('groups', 'prompt'), 'sample', 'fsdp'), parts along dimension 0
- query_grad: bfloat16 [4, 32, 512, 4096], P(('groups', 'prompt'), 'sample', 'fsdp'), parts along dimension 0
- completion_key_grad: float32 [4, 32, 512, 512], P(('groups', 'prompt'), 'sample', 'fsdp'), parts along dimension 0
- completion_value_grad: float32 [4, 32, 512, 512], P(('groups', 'prompt'), 'sample', 'fsdp'), parts along dimension 0
- shared_prompt_key_gradient: float32 [4, 128, 512], P(('groups', 'prompt'), ('sample', 'fsdp')), parts along dimension 0
- shared_prompt_value_gradient: float32 [4, 128, 512], P(('groups', 'prompt'), ('sample', 'fsdp')), parts along dimension 0
There are 2 independent parts, one for each index of `groups`. A program takes and returns all parts, laid end to end along the dimension named above; each array names one. Nothing has to cross between parts.
All inputs are finite; a program needn't handle non-finite values.
Results may differ from a plain program's by a relative error of at most 0.02.
Values may be sent and summed in bfloat16 or wider, within the bound.
A program may use at most 128 MiB of HBM per device.

v0:
```python
import jax
import jax.numpy as jnp
from jax import lax
from jax.sharding import PartitionSpec as P

HEAD_DIM = 128


def side_by_side(arrays, axis, dim, along):
    ends, at = ([], 0)
    for a in arrays[:-1]:
        at += a.shape[along]
        ends.append(at)
    both = jnp.concatenate(arrays, axis=along)
    return tuple(jnp.split(lax.all_gather(both, axis, axis=dim, tiled=True), ends, axis=along))


def in_blocks(value, dim, devices):
    before, after = (value.shape[:dim], value.shape[dim + 1 :])
    return jnp.moveaxis(value.reshape(*before, devices, -1, *after), dim, 0)


def sent_and_summed(value, axis, dim):
    devices = lax.axis_size(axis)
    pieces = lax.all_to_all(in_blocks(value, dim, devices), axis, 0, 0, tiled=True)
    return jnp.sum(pieces, axis=0)


def in_one_piece(arrays, axis, dim, along):
    widths = [a.shape[along] for a in arrays]
    both = jnp.concatenate(arrays, axis=along)
    filled = sent_and_summed(both, axis, dim)
    return tuple(jnp.split(filled, [sum(widths[:k]) for k in range(1, len(widths))], axis=along))


def sum_at_owner(value, axis, dim):
    pieces = in_blocks(value, dim, lax.axis_size(axis))
    arrived = lax.all_to_all(pieces, axis, split_axis=0, concat_axis=0, tiled=True)
    return arrived.astype(jnp.float32).sum(axis=0)


def sent_together(arrays, axis, dim, along):
    widths = [a.shape[along] for a in arrays]
    both = jnp.concatenate(arrays, axis=along)
    filled = sum_at_owner(both, axis, dim)
    return tuple(jnp.split(filled, [sum(widths[:k]) for k in range(1, len(widths))], axis=along))


def gather_prefix(prompt_keys, prompt_values):
    nearby = side_by_side((prompt_keys, prompt_values), "fsdp", 0, 1)
    return side_by_side((nearby[0], nearby[1]), "sample", 0, 1)


def reduce_prefix(key_terms, value_terms):
    partial_sums = in_one_piece((key_terms, value_terms), "sample", 0, 1)
    return in_one_piece((partial_sums[0], partial_sums[1]), "fsdp", 0, 1)


def shards(
    queries, completion_keys, completion_values, prompt_keys, prompt_values, output_grad, lengths
):
    query_rows = queries[0, 0]
    row_count = query_rows.shape[0]
    head_total = query_rows.shape[1] // HEAD_DIM
    group_count = prompt_keys.shape[2] // HEAD_DIM
    group_share = head_total // group_count
    group_width = group_share * HEAD_DIM
    softmax_scale = HEAD_DIM ** (-0.5)
    comp_span = row_count * lax.axis_size("fsdp")
    prefix_keys, prefix_values = gather_prefix(prompt_keys[0], prompt_values[0])
    own_keys, own_values = side_by_side(
        (completion_keys[0, 0], completion_values[0, 0]), "fsdp", 0, 1
    )
    prompt_span = prefix_keys.shape[0]
    all_keys = jnp.concatenate([prefix_keys, own_keys], 0)
    all_values = jnp.concatenate([prefix_values, own_values], 0)
    token_pos = lax.axis_index("fsdp") * row_count + jnp.arange(row_count, dtype=jnp.int32)
    key_pos = jnp.arange(prompt_span + comp_span, dtype=jnp.int32)
    visible = (key_pos[None, :] < prompt_span) | (
        key_pos[None, :] - prompt_span <= token_pos[:, None]
    )
    length = lengths[0, 0]
    token_weight = jnp.where(
        token_pos < length, jnp.float32(comp_span) / length.astype(jnp.float32), jnp.float32(0.0)
    )
    gradient_row_slice = (output_grad[0, 0].astype(jnp.float32) * token_weight[:, None]).astype(
        jnp.bfloat16
    )
    mixed_parts, query_parts = ([], [])
    prefix_key_terms, prompt_value_contrib, own_key_terms, own_value_terms = ([], [], [], [])
    for head_group in range(group_count):
        first_column = head_group * group_width
        query_block = query_rows[:, first_column : first_column + group_width].reshape(
            row_count, group_share, HEAD_DIM
        )
        grad_block = gradient_row_slice[:, first_column : first_column + group_width].reshape(
            row_count, group_share, HEAD_DIM
        )
        key_block = all_keys[:, head_group * HEAD_DIM : (head_group + 1) * HEAD_DIM]
        value_block = all_values[:, head_group * HEAD_DIM : (head_group + 1) * HEAD_DIM]
        scores = (
            jnp.einsum("trd,jd->rtj", query_block, key_block, preferred_element_type=jnp.float32)
            * softmax_scale
        )
        scores = jnp.where(visible[None], scores, -jnp.inf)
        maximum = jnp.max(scores, axis=-1, keepdims=True)
        exponent = jnp.exp(scores - maximum)
        inverse_total = 1.0 / jnp.sum(exponent, axis=-1, keepdims=True)
        attention = exponent * inverse_total
        attention_half = attention.astype(jnp.bfloat16)
        blended_output = jnp.einsum(
            "rtj,jd->trd", attention_half, value_block, preferred_element_type=jnp.float32
        ).astype(jnp.bfloat16)
        row_inner_product = jnp.sum(
            grad_block.astype(jnp.float32) * blended_output.astype(jnp.float32), axis=-1
        ).T
        prob_grad = jnp.einsum(
            "trd,jd->rtj", grad_block, value_block, preferred_element_type=jnp.float32
        )
        score_grad = (attention * (prob_grad - row_inner_product[:, :, None])).astype(jnp.bfloat16)
        query_grad = (
            jnp.einsum("rtj,jd->trd", score_grad, key_block, preferred_element_type=jnp.float32)
            * softmax_scale
        )
        key_grad = (
            jnp.einsum("rtj,trd->jd", score_grad, query_block, preferred_element_type=jnp.float32)
            * softmax_scale
        )
        value_grad = jnp.einsum(
            "rtj,trd->jd", attention_half, grad_block, preferred_element_type=jnp.float32
        )
        mixed_parts.append(blended_output.reshape(row_count, group_width))
        query_parts.append(query_grad.astype(jnp.bfloat16).reshape(row_count, group_width))
        prefix_key_terms.append(key_grad[:prompt_span])
        prompt_value_contrib.append(value_grad[:prompt_span])
        own_key_terms.append(key_grad[prompt_span:])
        own_value_terms.append(value_grad[prompt_span:])
    prefix_key_grad, prefix_value_grad = reduce_prefix(
        jnp.concatenate(prefix_key_terms, 1), jnp.concatenate(prompt_value_contrib, 1)
    )
    own_key_grad, own_value_grad = sent_together(
        (
            jnp.concatenate(own_key_terms, 1).astype(jnp.bfloat16),
            jnp.concatenate(own_value_terms, 1).astype(jnp.bfloat16),
        ),
        "fsdp",
        0,
        1,
    )
    attention_out = jnp.concatenate(mixed_parts, 1)[None, None]
    query_out = jnp.concatenate(query_parts, 1)[None, None]
    return (
        attention_out,
        query_out,
        own_key_grad[None, None],
        own_value_grad[None, None],
        prefix_key_grad[None],
        prefix_value_grad[None],
    )


def solution(mesh):
    in_specs = (
        P(("groups", "prompt"), "sample", "fsdp", None),
        P(("groups", "prompt"), "sample", "fsdp", None),
        P(("groups", "prompt"), "sample", "fsdp", None),
        P(("groups", "prompt"), ("sample", "fsdp"), None),
        P(("groups", "prompt"), ("sample", "fsdp"), None),
        P(("groups", "prompt"), "sample", "fsdp", None),
        P(("groups", "prompt"), "sample"),
    )
    out_specs = (
        P(("groups", "prompt"), "sample", "fsdp", None),
        P(("groups", "prompt"), "sample", "fsdp", None),
        P(("groups", "prompt"), "sample", "fsdp", None),
        P(("groups", "prompt"), "sample", "fsdp", None),
        P(("groups", "prompt"), ("sample", "fsdp"), None),
        P(("groups", "prompt"), ("sample", "fsdp"), None),
    )
    return jax.shard_map(shards, mesh=mesh, in_specs=in_specs, out_specs=out_specs, check_vma=False)
```

profile of v0, /device:TPU:40, one launch (start us, length us, event | category | flops | bytes accessed | tf_op | source)
XLA Modules:
  0.0 291.3 jit_solution(1914352032340905780)
XLA Ops:
  7.3 1.7 pad_maximum_fusion
  9.7 1.5 fusion.12
  11.3 12.8 %all-gather = bf16[4,1,1024]{2,1,0:T(2,128)(2,1)S(1)} all-gather(bf16[1,1,1024]{2,1,0:T(2,128)(2,1)S(1)} %maximum_bitcast_fusion.2), channel_id=1, replica_groups=mesh['groups'=2,'sample'=32,'fsdp'=4,'prompt'=2] {'fsdp'}, dimensions={0}, use_global_device_ids=true | all-gather | bytes 10240 | tf_op jit(solution)/shard_map/all_gather | solution.py:15
  24.1 95.9 %all-gather.1 = bf16[32,4,1024]{2,1,0:T(4,128)(2,1)S(1)} all-gather(bf16[1,4,1024]{2,1,0:T(4,128)(2,1)S(1)} %bitcast.323), channel_id=1, replica_groups=mesh['groups'=2,'sample'=32,'fsdp'=4,'prompt'=2] {'sample'}, dimensions={0}, use_global_device_ids=true | all-gather | bytes 270336 | tf_op jit(solution)/shard_map/all_gather | solution.py:15
  120.1 0.9 fusion.126
  121.0 1.1 copy.156
  122.1 1.9 copy.168
  124.0 0.8 copy.164
  124.8 0.8 copy.160
  125.7 0.8 copy.139
  126.9 1.3 fusion.128
  128.3 2.0 fusion.119
  131.0 2.1 fusion.140
  133.0 2.4 fusion.130
  135.4 2.4 fusion.137
  137.9 3.5 %multiply_reduce_fusion.3 = (f32[128,8]{0,1:T(8,128)S(1)}, bf16[128,8,128]{2,0,1:T(8,128)(2,1)}) fusion(bf16[128,1024]{0,1:T(8,128)(2,1)S(1)} %copy.156, f32[8,128]{1,0:T(8,128)S(1)} %broadcast_divide_fusion.3, f32[640,128,8]{1,0,2:T(8,128)} %fusion.119, pred[128,640]{0,1:T(8,128)(4,1)S(1)} %compare_or_fusion, bf16[512,512]{1,0:T(8,128)(2,1)S(1)} %get-tuple-element.15, ...), kind=kOutput, calls=%fused_computation.88 | convolution fusion | flops 172032640 | bytes 3891200 | tf_op jit(solution)/shard_map/rtj,jd->trd/dot_general | solution.py:111
  141.3 3.4 %convolution_bitcast_fusion.3 = f32[640,128]{1,0:T(8,128)} fusion(bf16[128,8,128]{0,2,1:T(8,128)(2,1)S(1)} %bitcast.303, f32[8,128]{1,0:T(8,128)S(1)} %broadcast_divide_fusion.3, f32[640,128,8]{1,0,2:T(8,128)} %fusion.119, pred[128,640]{0,1:T(8,128)(4,1)S(1)} %compare_or_fusion), kind=kOutput, calls=%fused_computation.62 | convolution fusion | flops 171050624 | bytes 3297280 | tf_op jit(solution)/shard_map/rtj,trd->jd/dot_general | solution.py:129
  144.7 2.4 fusion.11
  148.9 2.0 fusion.124
  150.9 2.4 fusion.131
  153.3 2.0 fusion.114
  155.3 2.4 fusion.134
  157.7 3.6 %multiply_reduce_fusion = (f32[128,8]{0,1:T(8,128)S(1)}, bf16[128,8,128]{2,0,1:T(8,128)(2,1)}) fusion(bf16[128,1024]{0,1:T(8,128)(2,1)} %copy.168, bf16[640,128,1]{1,0,2:T(8,128)(2,1)} %get-tuple-element.39, f32[8,128]{1,0:T(8,128)S(1)} %broadcast_divide_fusion, f32[640,128,8]{1,0,2:T(8,128)} %fusion.140, pred[128,640]{0,1:T(8,128)(4,1)S(1)} %compare_or_fusion), kind=kOutput, calls=%fused_computation.85 | convolution fusion | flops 171704960 | bytes 3399680 | tf_op jit(solution)/shard_map/rtj,jd->trd/dot_general | solution.py:111
  161.3 3.4 %convolution_bitcast_fusion = f32[640,128]{1,0:T(8,128)} fusion(bf16[128,8,128]{0,2,1:T(8,128)(2,1)S(1)} %bitcast.302, f32[8,128]{1,0:T(8,128)S(1)} %broadcast_divide_fusion, f32[640,128,8]{1,0,2:T(8,128)} %fusion.140, pred[128,640]{0,1:T(8,128)(4,1)S(1)} %compare_or_fusion), kind=kOutput, calls=%fused_computation.59 | convolution fusion | flops 171050624 | bytes 3297280 | tf_op jit(solution)/shard_map/rtj,trd->jd/dot_general | solution.py:129
  164.7 2.5 fusion.5
  169.1 1.0 slice.274
  170.0 1.6 slice.277
  172.3 3.7 %multiply_reduce_fusion.1 = (f32[128,8]{0,1:T(8,128)S(1)}, bf16[128,8,128]{2,0,1:T(8,128)(2,1)}) fusion(bf16[128,1024]{0,1:T(8,128)(2,1)} %copy.164, f32[8,128]{1,0:T(8,128)S(1)} %broadcast_divide_fusion.1, f32[640,128,8]{1,0,2:T(8,128)} %fusion.124, pred[128,640]{0,1:T(8,128)(4,1)} %copy-done.24, bf16[512,512]{1,0:T(8,128)(2,1)S(1)} %get-tuple-element.15, ...), kind=kOutput, calls=%fused_computation.86 | convolution fusion | flops 172032640 | bytes 3891200 | tf_op jit(solution)/shard_map/rtj,jd->trd/dot_general | solution.py:111
  176.0 3.4 %convolution_bitcast_fusion.1 = f32[640,128]{1,0:T(8,128)} fusion(bf16[128,8,128]{0,2,1:T(8,128)(2,1)S(1)} %bitcast.300, f32[8,128]{1,0:T(8,128)S(1)} %broadcast_divide_fusion.1, f32[640,128,8]{1,0,2:T(8,128)} %fusion.124, pred[128,640]{0,1:T(8,128)(4,1)} %copy-done.24), kind=kOutput, calls=%fused_computation.60 | convolution fusion | flops 171050624 | bytes 3297280 | tf_op jit(solution)/shard_map/rtj,trd->jd/dot_general | solution.py:129
  179.5 2.4 fusion.7
  181.9 1.1 copy-done.1
  184.2 1.0 slice.275
  185.2 3.5 %multiply_reduce_fusion.2 = (f32[128,8]{0,1:T(8,128)S(1)}, bf16[128,8,128]{2,0,1:T(8,128)(2,1)}) fusion(bf16[128,1024]{0,1:T(8,128)(2,1)S(1)} %copy-done.8, f32[8,128]{1,0:T(8,128)S(1)} %broadcast_divide_fusion.2, f32[640,128,8]{1,0,2:T(8,128)} %fusion.114, pred[128,640]{0,1:T(8,128)(4,1)} %copy-done.24, bf16[512,512]{1,0:T(8,128)(2,1)S(1)} %get-tuple-element.15, ...), kind=kOutput, calls=%fused_computation.87 | convolution fusion | flops 172032640 | bytes 3891200 | tf_op jit(solution)/shard_map/rtj,jd->trd/dot_general | solution.py:111
  188.7 3.4 %convolution_bitcast_fusion.2 = f32[640,128]{1,0:T(8,128)} fusion(bf16[128,8,128]{0,2,1:T(8,128)(2,1)S(1)} %bitcast.297, f32[8,128]{1,0:T(8,128)S(1)} %broadcast_divide_fusion.2, f32[640,128,8]{1,0,2:T(8,128)} %fusion.114, pred[128,640]{0,1:T(8,128)(4,1)} %copy-done.24), kind=kOutput, calls=%fused_computation.61 | convolution fusion | flops 171050624 | bytes 3297280 | tf_op jit(solution)/shard_map/rtj,trd->jd/dot_general | solution.py:129
  192.1 2.3 fusion.9
  194.4 1.1 copy-done.3
  196.6 1.5 slice_dynamic-update-slice_fusion.5
  198.1 1.5 slice_dynamic-update-slice_fusion.4
  199.5 1.0 slice.276
  205.2 4.0 %all-to-all-start = ((bf16[4,128,1024]{2,1,0:T(8,128)(2,1)}), bf16[4,128,1024]{2,1,0:T(8,128)(2,1)S(1)}, u32[]{:S(2)}, u32[]{:S(2)}) async-start(bf16[4,128,1024]{2,1,0:T(8,128)(2,1)} %constant_dynamic-update-slice_fusion), calls=%async_computation | async-start | bytes 2097152 | tf_op jit(solution)/shard_map/all_to_all | solution.py:38
  209.1 1.5 slice_dynamic-update-slice_fusion.3
  210.6 1.5 slice_dynamic-update-slice_fusion.2
  212.1 1.5 slice_dynamic-update-slice_fusion.1
  213.5 1.5 slice_dynamic-update-slice_fusion
  215.0 2.0 reshape.188
  217.0 3.0 %all-to-all-done = bf16[4,128,1024]{2,1,0:T(8,128)(2,1)S(1)} async-done(((bf16[4,128,1024]{2,1,0:T(8,128)(2,1)}), bf16[4,128,1024]{2,1,0:T(8,128)(2,1)S(1)}, u32[]{:S(2)}, u32[]{:S(2)}) %all-to-all-start) | async-done | bytes 1048608 | tf_op jit(solution)/shard_map/all_to_all | solution.py:38
  220.0 5.4 %all-to-all-start.1 = ((f32[32,4,1024]{2,1,0:T(4,128)}), f32[32,4,1024]{2,1,0:T(4,128)}, u32[]{:S(2)}, u32[]{:S(2)}) async-start(f32[32,4,1024]{2,1,0:T(4,128)} %reshape.188), calls=%async_computation.1 | async-start | bytes 1048576 | tf_op jit(solution)/shard_map/all_to_all | solution.py:25
  225.5 0.8 copy.155
  226.3 1.1 fusion.32
  227.4 1.9 copy.175
  229.3 1.1 copy.152
  230.4 1.7 fusion.29
  232.1 0.9 copy.172
  233.0 1.8 copy.154
  235.2 0.8 copy.174
  236.1 1.8 fusion.30
  238.0 1.1 copy.153
  239.1 1.0 maximum_bitcast_fusion.1
  240.2 1.0 maximum_bitcast_fusion
  241.4 32.1 %all-to-all-done.1 = f32[32,4,1024]{2,1,0:T(4,128)} async-done(((f32[32,4,1024]{2,1,0:T(4,128)}), f32[32,4,1024]{2,1,0:T(4,128)}, u32[]{:S(2)}, u32[]{:S(2)}) %all-to-all-start.1) | async-done | bytes 524320 | tf_op jit(solution)/shard_map/all_to_all | solution.py:25
  273.5 1.1 reduce_sum.110
  275.2 3.3 %all-to-all-start.2 = ((f32[4,1,1024]{2,1,0:T(1,128)}), f32[4,1,1024]{2,1,0:T(1,128)S(1)}, u32[]{:S(2)}, u32[]{:S(2)}) async-start(f32[4,1,1024]{2,1,0:T(1,128)} %reshape.189), calls=%async_computation.2 | async-start | bytes 32768 | tf_op jit(solution)/shard_map/all_to_all | solution.py:25
  278.6 0.8 slice_bitcast_fusion
  279.4 4.4 %all-to-all-done.2 = f32[4,1,1024]{2,1,0:T(1,128)S(1)} async-done(((f32[4,1,1024]{2,1,0:T(1,128)}), f32[4,1,1024]{2,1,0:T(1,128)S(1)}, u32[]{:S(2)}, u32[]{:S(2)}) %all-to-all-start.2) | async-done | bytes 16416 | tf_op jit(solution)/shard_map/all_to_all | solution.py:25
  (94 shorter events, 14.7 us)
Async XLA Ops:
  7.2 4.1 %copy-start.25 = (bf16[1,1,512]{2,1,0:T(2,128)(2,1)S(1)}, bf16[1,1,512]{2,1,0:T(2,128)(2,1)}, u32[]{:S(2)}) copy-start(bf16[1,1,512]{2,1,0:T(2,128)(2,1)} %param.11) | copy-start | bytes 3076
  7.2 4.1 %copy-start.26 = (bf16[1,1,512]{2,1,0:T(2,128)(2,1)S(1)}, bf16[1,1,512]{2,1,0:T(2,128)(2,1)}, u32[]{:S(2)}) copy-start(bf16[1,1,512]{2,1,0:T(2,128)(2,1)} %param.10) | copy-start | bytes 3076
  7.2 119.7 %all-gather.4.cloned.1.call-start = ((), (), s32[]{:S(2)}) async-start(), calls=%async_computation.3 | async-start | bytes 1310720 | tf_op jit(solution)/shard_map/all_gather | solution.py:15
  11.2 114.4 %copy-start.12 = (bf16[1,1,128,4096]{3,2,1,0:T(8,128)(2,1)S(1)}, bf16[1,1,128,4096]{3,2,1,0:T(8,128)(2,1)}, u32[]{:S(2)}) copy-start(bf16[1,1,128,4096]{3,2,1,0:T(8,128)(2,1)} %param.7) | copy-start | bytes 3145732
  122.1 19.2 %copy-start.11 = (bf16[128,1024]{0,1:T(8,128)(2,1)}, bf16[128,1024]{0,1:T(8,128)(2,1)S(1)}, u32[]{:S(2)}) copy-start(bf16[128,1024]{0,1:T(8,128)(2,1)S(1)} %copy.156) | copy-start | bytes 786436
  126.8 34.5 %copy-start.24 = (pred[128,640]{0,1:T(8,128)(4,1)}, pred[128,640]{0,1:T(8,128)(4,1)S(1)}, u32[]{:S(2)}) copy-start(pred[128,640]{0,1:T(8,128)(4,1)S(1)} %compare_or_fusion) | copy-start | bytes 245764
  126.9 8.5 %copy-start.4 = (bf16[128,1024]{0,1:T(8,128)(2,1)}, bf16[128,1024]{0,1:T(8,128)(2,1)S(1)}, u32[]{:S(2)}) copy-start(bf16[128,1024]{0,1:T(8,128)(2,1)S(1)} %get-tuple-element.10) | copy-start | bytes 786436
  131.0 4.5 %copy-start.6 = (bf16[640,128,1]{1,0,2:T(8,128)(2,1)}, bf16[640,128,1]{1,0,2:T(8,128)(2,1)S(1)}, u32[]{:S(2)}) copy-start(bf16[640,128,1]{1,0,2:T(8,128)(2,1)S(1)} %get-tuple-element.38) | copy-start | bytes 491524
  144.7 2.4 copy-start.5
  147.1 10.6 %copy-start = (bf16[8,128,640]{1,2,0:T(8,128)(2,1)}, bf16[8,128,640]{1,2,0:T(8,128)(2,1)S(1)}, u32[]{:S(2)}) copy-start(bf16[8,128,640]{1,2,0:T(8,128)(2,1)S(1)} %fusion.11) | copy-start | bytes 3932164
  157.7 3.6 %copy-start.10 = (bf16[128,1024]{0,1:T(8,128)(2,1)S(1)}, bf16[128,1024]{0,1:T(8,128)(2,1)}, u32[]{:S(2)}) copy-start(bf16[128,1024]{0,1:T(8,128)(2,1)} %copy.168) | copy-start | bytes 786436
  164.7 7.0 %copy-start.22 = (bf16[512,128]{1,0:T(8,128)(2,1)S(1)}, bf16[512,128]{1,0:T(8,128)(2,1)}, u32[]{:S(2)}) copy-start(bf16[512,128]{1,0:T(8,128)(2,1)} %slice.281) | copy-start | bytes 393220
  167.7 0.7 copy-start.18
  168.4 7.7 %copy-start.9 = (bf16[128,1024]{0,1:T(8,128)(2,1)S(1)}, bf16[128,1024]{0,1:T(8,128)(2,1)}, u32[]{:S(2)}) copy-start(bf16[128,1024]{0,1:T(8,128)(2,1)} %copy.164) | copy-start | bytes 786436
  179.5 5.7 %copy-start.8 = (bf16[128,1024]{0,1:T(8,128)(2,1)S(1)}, bf16[128,1024]{0,1:T(8,128)(2,1)}, u32[]{:S(2)}) copy-start(bf16[128,1024]{0,1:T(8,128)(2,1)} %copy.160) | copy-start | bytes 786436
  181.8 1.1 copy-start.1
  183.5 0.7 copy-start.19
  194.3 1.1 copy-start.3
  195.4 6.4 %copy-start.21 = (bf16[512,128]{1,0:T(8,128)(2,1)S(1)}, bf16[512,128]{1,0:T(8,128)(2,1)}, u32[]{:S(2)}) copy-start(bf16[512,128]{1,0:T(8,128)(2,1)} %slice.278) | copy-start | bytes 393220
  195.4 7.1 %copy-start.20 = (bf16[512,128]{1,0:T(8,128)(2,1)S(1)}, bf16[512,128]{1,0:T(8,128)(2,1)}, u32[]{:S(2)}) copy-start(bf16[512,128]{1,0:T(8,128)(2,1)} %slice.277) | copy-start | bytes 393220
  203.8 21.6 %copy-start.23 = (bf16[128,8,128]{2,0,1:T(8,128)(2,1)S(1)}, bf16[128,8,128]{2,0,1:T(8,128)(2,1)}, u32[]{:S(2)}) copy-start(bf16[128,8,128]{2,0,1:T(8,128)(2,1)} %get-tuple-element.31) | copy-start | bytes 786436
  205.2 21.1 %copy-start.7 = (bf16[640,128,1]{1,0,2:T(8,128)(2,1)S(1)}, bf16[640,128,1]{1,0,2:T(8,128)(2,1)}, u32[]{:S(2)}) copy-start(bf16[640,128,1]{1,0,2:T(8,128)(2,1)} %copy-done.6) | copy-start | bytes 491524
  205.2 14.8 %all-to-all-start = ((bf16[4,128,1024]{2,1,0:T(8,128)(2,1)}), bf16[4,128,1024]{2,1,0:T(8,128)(2,1)S(1)}, u32[]{:S(2)}, u32[]{:S(2)}) async-start(bf16[4,128,1024]{2,1,0:T(8,128)(2,1)} %constant_dynamic-update-slice_fusion), calls=%async_computation | async-start | bytes 2097152 | tf_op jit(solution)/shard_map/all_to_all | solution.py:38
  220.0 53.5 %all-to-all-start.1 = ((f32[32,4,1024]{2,1,0:T(4,128)}), f32[32,4,1024]{2,1,0:T(4,128)}, u32[]{:S(2)}, u32[]{:S(2)}) async-start(f32[32,4,1024]{2,1,0:T(4,128)} %reshape.188), calls=%async_computation.1 | async-start | bytes 1048576 | tf_op jit(solution)/shard_map/all_to_all | solution.py:25
  227.4 7.4 %copy-start.2 = (bf16[8,128,640]{1,2,0:T(8,128)(2,1)S(1)}, bf16[8,128,640]{1,2,0:T(8,128)(2,1)}, u32[]{:S(2)}) copy-start(bf16[8,128,640]{1,2,0:T(8,128)(2,1)} %copy-done.1) | copy-start | bytes 3932164
  235.2 3.9 %copy-start.14 = (bf16[128,1024]{1,0:T(8,128)(2,1)S(1)}, bf16[128,1024]{1,0:T(8,128)(2,1)}, u32[]{:S(2)}) copy-start(bf16[128,1024]{1,0:T(8,128)(2,1)} %copy.175) | copy-start | bytes 786436
  235.2 3.9 %copy-start.16 = (bf16[128,1024]{1,0:T(8,128)(2,1)S(1)}, bf16[128,1024]{1,0:T(8,128)(2,1)}, u32[]{:S(2)}) copy-start(bf16[128,1024]{1,0:T(8,128)(2,1)} %copy.172) | copy-start | bytes 786436
  236.1 3.1 %copy-start.17 = (bf16[128,1024]{1,0:T(8,128)(2,1)S(1)}, bf16[128,1024]{1,0:T(8,128)(2,1)}, u32[]{:S(2)}) copy-start(bf16[128,1024]{1,0:T(8,128)(2,1)} %copy.174) | copy-start | bytes 786436
  236.1 4.1 %copy-start.13 = (bf16[128,1024]{1,0:T(8,128)(2,1)S(1)}, bf16[128,1024]{1,0:T(8,128)(2,1)}, u32[]{:S(2)}) copy-start(bf16[128,1024]{1,0:T(8,128)(2,1)} %copy.155) | copy-start | bytes 786436
  236.1 4.1 %copy-start.15 = (bf16[128,1024]{1,0:T(8,128)(2,1)S(1)}, bf16[128,1024]{1,0:T(8,128)(2,1)}, u32[]{:S(2)}) copy-start(bf16[128,1024]{1,0:T(8,128)(2,1)} %copy.154) | copy-start | bytes 786436
  275.2 8.6 %all-to-all-start.2 = ((f32[4,1,1024]{2,1,0:T(1,128)}), f32[4,1,1024]{2,1,0:T(1,128)S(1)}, u32[]{:S(2)}, u32[]{:S(2)}) async-start(f32[4,1,1024]{2,1,0:T(1,128)} %reshape.189), calls=%async_computation.2 | async-start | bytes 32768 | tf_op jit(solution)/shard_map/all_to_all | solution.py:25
Sparse Core Ops, SparseCore 0:
  10.7 64.4 all-gather.3
where the time goes:
time: 293 us; the launch traced here: 291 us
  blocking collectives  109 us (37%)
  matrix products  62 us (21%)
  local copies, waits for them, and re-layouts  45.4 us (15%)
  waiting for transfers between devices  39.6 us (14%)
  between operations  15.2 us (5%)
  starting transfers between devices  12.8 us (4%)
  other arithmetic  7.58 us (3%)
    all_gather x2, blocking collectives, side_by_side(): lax.all_gather(both, axis, axis=dim, tiled=True)  109 us
    all_to_all x2, waiting for transfers between devices, sent_and_summed(): lax.all_to_all(in_blocks(value, dim, devices), axis, 0, 0, tiled=True)  36.5 us
    unnamed x71, local copies, waits for them, and re-layouts  17.9 us
    dot_general x4, matrix products, shards(): jnp.einsum('rtj,jd->trd', attention_half, value_block, preferred_element_...  14.2 us
    dot_general x4, matrix products, shards(): jnp.einsum('rtj,trd->jd', attention_half, grad_block, preferred_element_t...  13.6 us
    sub x4, matrix products, shards(): exponent = jnp.exp(scores - maximum)  9.61 us
    dot_general x4, matrix products, shards(): jnp.einsum('trd,jd->rtj', grad_block, value_block, preferred_element_type...  9.48 us
    all_to_all x2, starting transfers between devices, sent_and_summed(): lax.all_to_all(in_blocks(value, dim, devices), axis, 0, 0, tiled=True)  8.76 us
  transfers between devices with their start and end apart: 4, of which 3 were waited for; matrix products, arithmetic and copies ran while one was open for 11% of the time, Pallas kernels for 0%

commit v1 on v0

v1 whole, which is shorter than its diff:
```python
import functools
import math

import jax
import jax.numpy as jnp
from jax import lax
from jax.experimental import pallas as pl
from jax.experimental.pallas import tpu as pltpu
from jax.sharding import PartitionSpec as P

HEAD_DIM = 128
TILE = 256
MESH = pl.DeviceIdType.MESH
F32 = jnp.float32
BF16 = jnp.bfloat16
NT = (((1,), (1,)), ((), ()))
NN = (((1,), (0,)), ((), ()))


def dot(a, b, dims=NN):
    return lax.dot_general(a, b, dims, preferred_element_type=F32)


def kernel(
    nz,
    nx,
    queries,
    comp_k,
    comp_v,
    prompt_k,
    prompt_v,
    out_grad,
    lengths,
    out,
    query_grad,
    comp_k_grad,
    comp_v_grad,
    prompt_k_grad,
    prompt_v_grad,
    q_s,
    g_s,
    kv,
    kvt,
    rows,
    rows32,
    e_s,
    dp_s,
    o_s,
    dq_s,
    stat,
    blockmax,
    p_half,
    ds_half,
    o_half,
    dq_half,
    csend,
    crecv,
    cown,
    cstage,
    xsend,
    xown,
    xrecv,
    zf,
    zsend,
    zrecv,
    pstage,
    in_sem,
    kvin_sem,
    out_sem,
    gout_sem,
    r1_send,
    r1_recv,
    r2_send,
    r2_recv,
    rx_send,
    rx_recv,
    kv_send,
    kv_recv,
    x_send,
    x_recv,
    z_send,
    z_recv,
    c_send,
    c_recv,
):
    z = lax.axis_index("sample")
    x = lax.axis_index("fsdp")
    count = comp_k.shape[2]
    groups = comp_k.shape[3] // HEAD_DIM
    heads = queries.shape[3] // HEAD_DIM
    share = heads // groups
    wide = share * count
    reach = nz // 4
    scale = HEAD_DIM**-0.5
    fold = scale * math.log2(math.e)
    last = nx
    key_count = nz * nx

    def at_z(d):
        return {"sample": lax.rem(z + (d + nz) % nz, nz)}

    def at_x(d):
        return {"fsdp": lax.rem(x + d, nx)}

    def remote(src, dst, send, recv, to):
        return pltpu.make_async_remote_copy(
            src_ref=src, dst_ref=dst, send_sem=send, recv_sem=recv, device_id=to, device_id_type=MESH
        )

    own_kv = [
        pltpu.make_async_copy(comp_k.at[0, 0], kv.at[x, 0], kvin_sem.at[0]),
        pltpu.make_async_copy(comp_v.at[0, 0], kv.at[x, 1], kvin_sem.at[1]),
    ]
    for c in own_kv:
        c.start()

    @pl.loop(0, groups)
    def _(g):
        for h in range(share):
            head = g * share + h
            cols = pl.ds(pl.multiple_of(head * HEAD_DIM, HEAD_DIM), HEAD_DIM)
            dst = pl.ds(pl.multiple_of(head * count, count), count)
            pltpu.make_async_copy(queries.at[0, 0, :, cols], q_s.at[dst], in_sem.at[0, g]).start()
            pltpu.make_async_copy(out_grad.at[0, 0, :, cols], g_s.at[dst], in_sem.at[1, g]).start()

    for k, ref in enumerate((prompt_k, prompt_v)):
        row = ref[0].astype(F32)
        for g in range(groups):
            pstage[k * groups + g : k * groups + g + 1, :] = row[:, g * HEAD_DIM : (g + 1) * HEAD_DIM]
    rows[0, 0] = pstage[...].astype(BF16)

    barrier = pltpu.get_barrier_semaphore()
    near = [d for d in range(1, reach + 1)] + [-d for d in range(1, reach + 1)]
    for d in near:
        pl.semaphore_signal(barrier, inc=1, device_id=at_z(d), device_id_type=MESH)
    for d in range(1, nx):
        pl.semaphore_signal(barrier, inc=1, device_id=at_x(d), device_id_type=MESH)

    def turn(b):
        for part in range(2):
            for g in range(groups):
                cols = slice(g * HEAD_DIM, (g + 1) * HEAD_DIM)
                kvt[b, part, cols, :] = kv[b, part, :, cols].astype(F32).T.astype(BF16)

    def forward(b, g, first):
        cols = pl.ds(pl.multiple_of(g * HEAD_DIM, HEAD_DIM), HEAD_DIM)
        keys = kv[b, 0, :, cols]
        values = kv[b, 1, :, cols]
        values_t = kvt[b, 1, cols, :]
        slot = g * (nx + 1) + b
        for t in range(wide // TILE):
            at = slice(t * TILE, (t + 1) * TILE)
            src = pl.ds(pl.multiple_of(g * wide + t * TILE, TILE), TILE)
            s = dot(keys, q_s[src, :], NT)
            if first:
                key = lax.broadcasted_iota(jnp.int32, s.shape, 0)
                token = lax.broadcasted_iota(jnp.int32, s.shape, 1) % count
                s = jnp.where(key <= token, s, -1e30)
            top = jnp.max(s, axis=0, keepdims=True)
            if not first:
                before = stat[g, 0:1, at]
                top = jnp.maximum(top, before)
            e = jnp.exp2((s - top) * fold)
            total = jnp.sum(e, axis=0, keepdims=True)
            dp = dot(values, g_s[src, :], NT)
            mean = jnp.sum(e * dp, axis=0, keepdims=True)
            o = dot(values_t, e.astype(BF16))
            if not first:
                old = jnp.exp2((before - top) * fold)
                total += old * stat[g, 1:2, at]
                mean += old * stat[g, 2:3, at]
                o += old * o_s[g, :, at]
            stat[g, 0:1, at] = top
            stat[g, 1:2, at] = total
            stat[g, 2:3, at] = mean
            o_s[g, :, at] = o
            e_s[slot, :, at] = e
            dp_s[slot, :, at] = dp
            blockmax[slot, 0:1, at] = top

    def backward(b, g, first):
        cols = pl.ds(pl.multiple_of(g * HEAD_DIM, HEAD_DIM), HEAD_DIM)
        keys_t = kvt[b, 0, cols, :]
        slot = g * (nx + 1) + b
        for t in range(wide // TILE):
            at = slice(t * TILE, (t + 1) * TILE)
            factor = jnp.exp2((blockmax[slot, 0:1, at] - stat[g, 0:1, at]) * fold) * stat[g, 1:2, at]
            p = e_s[slot, :, at] * factor
            ds = (p * (dp_s[slot, :, at] - stat[g, 2:3, at])).astype(BF16)
            p_half[:, at] = p.astype(BF16)
            ds_half[:, at] = ds
            dq = dot(keys_t, ds)
            if first:
                dq_s[g, :, at] = dq
            else:
                dq_s[g, :, at] += dq
        src = pl.ds(pl.multiple_of(g * wide, wide), wide)
        return dot(ds_half[...], q_s[src, :]) * scale, dot(p_half[...], g_s[src, :])

    def flush(source, staged, target, g, sem):
        for t in range(wide // TILE):
            at = slice(t * TILE, (t + 1) * TILE)
            dst = pl.ds(pl.multiple_of(g * wide + t * TILE, TILE), TILE)
            staged[dst, :] = source(at).T.astype(BF16)
        for h in range(share):
            head = g * share + h
            cols = pl.ds(pl.multiple_of(head * HEAD_DIM, HEAD_DIM), HEAD_DIM)
            src = pl.ds(pl.multiple_of(head * count, count), count)
            pltpu.make_async_copy(staged.at[src], target.at[0, 0, :, cols], sem).start()

    for c in own_kv:
        c.wait()
    turn(x)
    token = lax.broadcasted_iota(jnp.int32, (count, HEAD_DIM), 0) + x * count
    length = jnp.full((count, HEAD_DIM), lengths[0, 0], jnp.int32)
    weight = jnp.where(token < length, F32(count * nx) / length.astype(F32), 0.0)

    @pl.loop(0, groups)
    def _(g):
        src = pl.ds(pl.multiple_of(g * wide, wide), wide)
        pltpu.make_async_copy(q_s.at[src], q_s.at[src], in_sem.at[0, g]).wait()
        pltpu.make_async_copy(g_s.at[src], g_s.at[src], in_sem.at[1, g]).wait()
        for h in range(share):
            at = pl.ds(pl.multiple_of((g * share + h) * count, count), count)
            g_s[at, :] = (g_s[at, :].astype(F32) * weight).astype(BF16)
        forward(x, g, True)

    pl.semaphore_wait(barrier, len(near) + nx - 1)

    first_leg = {
        d: remote(
            rows.at[0, 0], rows.at[0, (nz - d) % nz], r1_send.at[n], r1_recv.at[n], at_z(d)
        )
        for n, d in enumerate(near)
    }
    for d in sorted(near, key=abs, reverse=True):
        first_leg[d].start()

    def kv_copy(d):
        return remote(kv.at[x], kv.at[x], kv_send.at[d - 1], kv_recv.at[d - 1], at_x(d))

    for d in range(1, nx):

        @pl.when(x + d < nx)
        def _(d=d):
            kv_copy(d).start()

    second_leg = []
    for e in range(1, reach + 1):
        first_leg[-e].wait_recv()
        c = remote(
            rows.at[0, e], rows.at[0, reach + e], r2_send.at[0, e - 1], r2_recv.at[0, e - 1], at_z(-reach)
        )
        c.start()
        second_leg.append(c)
        first_leg[e].wait_recv()
        if e < reach:
            c = remote(
                rows.at[0, nz - e],
                rows.at[0, nz - reach - e],
                r2_send.at[1, e - 1],
                r2_recv.at[1, e - 1],
                at_z(reach),
            )
            c.start()
            second_leg.append(c)

    def to_columns(part, begin, end):
        return [
            remote(
                rows.at[0, begin:end],
                rows.at[nx - d, begin:end],
                rx_send.at[part, d - 1],
                rx_recv.at[part, d - 1],
                at_x(d),
            )
            for d in range(1, nx)
        ]

    column_legs = to_columns(0, 0, reach + 1) + to_columns(1, nz - reach, nz)
    for c in column_legs:
        c.start()

    @pl.loop(0, x)
    def _(n):
        d = n + 1
        b = x - d
        remote(kv.at[b], kv.at[b], kv_send.at[n], kv_recv.at[n], at_x(1)).wait_recv()
        turn(b)

        @pl.loop(0, groups)
        def _(g):
            forward(b, g, False)

    for c in second_leg:
        c.wait_recv()
    final_legs = to_columns(2, reach + 1, nz - reach)
    for c in final_legs:
        c.start()
    column_legs += final_legs
    for c in column_legs:
        c.wait_recv()

    rows32[...] = rows[...].reshape(key_count, 2 * groups, HEAD_DIM).astype(F32)
    for part in range(2):
        for g in range(groups):
            cols = slice(g * HEAD_DIM, (g + 1) * HEAD_DIM)
            block = rows32[:, part * groups + g, :]
            kv[last, part, :, cols] = block.astype(BF16)
            kvt[last, part, cols, :] = block.T.astype(BF16)

    def x_copy(g, d):
        return remote(
            xsend.at[g, d], xrecv.at[g, nx - d], x_send.at[g, d - 1], x_recv.at[g, d - 1], at_x(d)
        )

    @pl.loop(0, groups)
    def _(g):
        forward(last, g, False)
        inverse = 1.0 / stat[g, 1:2, :]
        stat[g, 1:2, :] = inverse
        stat[g, 2:3, :] = stat[g, 2:3, :] * inverse
        both = backward(last, g, True)
        for part in range(2):
            xown[g, part] = both[part][:nz]
            for d in range(1, nx):
                xsend[g, d, part] = both[part][d * nz : (d + 1) * nz].astype(BF16)
        for d in range(1, nx):
            x_copy(g, d).start()
        flush(lambda at: o_s[g, :, at] * stat[g, 1:2, at], o_half, out, g, out_sem.at[0])

    def c_copy(b, g, d):
        return remote(
            csend.at[b, g], crecv.at[d - 1, g], c_send.at[b, g], c_recv.at[d - 1, g], {"fsdp": b}
        )

    def completion_backward(b):
        @pl.loop(0, groups)
        def _(g):
            both = backward(b, g, False)

            @pl.when(b < x)
            def _():
                for part in range(2):
                    csend[b, g, part] = both[part].astype(BF16)
                c_copy(b, g, x - b).start()

            @pl.when(b == x)
            def _():
                for part in range(2):
                    cown[g, part] = both[part]

    completion_backward(0)

    for g in range(groups):
        for d in range(1, nx):
            x_copy(g, d).wait_recv()
    for g in range(groups):
        for part in range(2):
            total = xown[g, part]
            for d in range(1, nx):
                total += xrecv[g, d, part].astype(F32)
            zf[:, part * groups + g, :] = total
    zsend[...] = zf[...].astype(BF16)

    def z_copy(s):
        return remote(zsend.at[s], zrecv.at[nz - s], z_send, z_recv, at_z(s))

    for s in sorted(range(1, nz), key=lambda s: min(s, nz - s), reverse=True):
        z_copy(s).start()

    @pl.loop(1, x + 1)
    def _(b):
        completion_backward(b)

    @pl.loop(0, groups)
    def _(g):
        flush(lambda at: dq_s[g, :, at] * scale, dq_half, query_grad, g, out_sem.at[1])

    for d in range(1, nx):

        @pl.when(x + d < nx)
        def _(d=d):
            for g in range(groups):
                remote(
                    csend.at[0, g], crecv.at[d - 1, g], c_send.at[0, g], c_recv.at[d - 1, g], at_x(d)
                ).wait_recv()
                for part in range(2):
                    cown[g, part] += crecv[d - 1, g, part].astype(F32)

    for part in range(2):
        for g in range(groups):
            cstage[part, :, g * HEAD_DIM : (g + 1) * HEAD_DIM] = cown[g, part]
    grads_out = [
        pltpu.make_async_copy(cstage.at[0], comp_k_grad.at[0, 0], gout_sem.at[0]),
        pltpu.make_async_copy(cstage.at[1], comp_v_grad.at[0, 0], gout_sem.at[1]),
    ]
    for c in grads_out:
        c.start()

    pltpu.make_async_copy(zrecv.at[1:nz], zrecv.at[1:nz], z_recv).wait()
    total = zf[0]
    for s in range(1, nz):
        total += zrecv[s].astype(F32)
    for k, ref in enumerate((prompt_k_grad, prompt_v_grad)):
        for g in range(groups):
            ref[0, :, g * HEAD_DIM : (g + 1) * HEAD_DIM] = total[k * groups + g : k * groups + g + 1, :]

    for c in list(first_leg.values()) + second_leg + column_legs:
        c.wait_send()
    for d in range(1, nx):

        @pl.when(x + d < nx)
        def _(d=d):
            kv_copy(d).wait_send()

        for g in range(groups):
            x_copy(g, d).wait_send()
    pltpu.make_async_copy(zsend.at[1:nz], zsend.at[1:nz], z_send).wait()

    @pl.loop(0, x)
    def _(b):
        for g in range(groups):
            remote(
                csend.at[b, g], crecv.at[0, g], c_send.at[b, g], c_recv.at[0, g], at_x(1)
            ).wait_send()

    pltpu.make_async_copy(o_half, o_half, out_sem.at[0]).wait()
    pltpu.make_async_copy(dq_half, dq_half, out_sem.at[1]).wait()
    for c in grads_out:
        c.wait()


def solution(mesh):
    nz, nx = mesh.shape["sample"], mesh.shape["fsdp"]

    def shards(queries, comp_k, comp_v, prompt_k, prompt_v, output_grad, lengths):
        count, width = queries.shape[2:]
        kv_width = comp_k.shape[3]
        groups = kv_width // HEAD_DIM
        heads = width // HEAD_DIM
        wide = heads // groups * count
        key_count = nz * nx
        reach = nz // 4
        blocks = nx + 1
        anywhere = pl.BlockSpec(memory_space=pl.ANY)
        vmem = pl.BlockSpec(memory_space=pltpu.VMEM)
        smem = pl.BlockSpec(memory_space=pltpu.SMEM)
        dma = pltpu.SemaphoreType.DMA
        one = jax.ShapeDtypeStruct
        return pl.pallas_call(
            functools.partial(kernel, nz, nx),
            out_shape=(
                one(queries.shape, BF16),
                one(queries.shape, BF16),
                one(comp_k.shape, F32),
                one(comp_k.shape, F32),
                one(prompt_k.shape, F32),
                one(prompt_k.shape, F32),
            ),
            in_specs=[anywhere, anywhere, anywhere, vmem, vmem, anywhere, smem],
            out_specs=(anywhere, anywhere, anywhere, anywhere, vmem, vmem),
            scratch_shapes=[
                pltpu.VMEM((heads * count, HEAD_DIM), BF16),
                pltpu.VMEM((heads * count, HEAD_DIM), BF16),
                pltpu.VMEM((blocks, 2, count, kv_width), BF16),
                pltpu.VMEM((blocks, 2, kv_width, count), BF16),
                pltpu.VMEM((nx, nz, 2 * groups, HEAD_DIM), BF16),
                pltpu.VMEM((key_count, 2 * groups, HEAD_DIM), F32),
                pltpu.VMEM((groups * blocks, count, wide), F32),
                pltpu.VMEM((groups * blocks, count, wide), F32),
                pltpu.VMEM((groups, HEAD_DIM, wide), F32),
                pltpu.VMEM((groups, HEAD_DIM, wide), F32),
                pltpu.VMEM((groups, 8, wide), F32),
                pltpu.VMEM((groups * blocks, 1, wide), F32),
                pltpu.VMEM((count, wide), BF16),
                pltpu.VMEM((count, wide), BF16),
                pltpu.VMEM((heads * count, HEAD_DIM), BF16),
                pltpu.VMEM((heads * count, HEAD_DIM), BF16),
                pltpu.VMEM((nx, groups, 2, count, HEAD_DIM), BF16),
                pltpu.VMEM((nx - 1, groups, 2, count, HEAD_DIM), BF16),
                pltpu.VMEM((groups, 2, count, HEAD_DIM), F32),
                pltpu.VMEM((2, count, kv_width), F32),
                pltpu.VMEM((groups, nx, 2, nz, HEAD_DIM), BF16),
                pltpu.VMEM((groups, 2, nz, HEAD_DIM), F32),
                pltpu.VMEM((groups, nx, 2, nz, HEAD_DIM), BF16),
                pltpu.VMEM((nz, 2 * groups, HEAD_DIM), F32),
                pltpu.VMEM((nz, 2 * groups, HEAD_DIM), BF16),
                pltpu.VMEM((nz, 2 * groups, HEAD_DIM), BF16),
                pltpu.VMEM((2 * groups, HEAD_DIM), F32),
                dma((2, groups)),
                dma((2,)),
                dma((2,)),
                dma((2,)),
                dma((2 * reach,)),
                dma((2 * reach,)),
                dma((2, reach)),
                dma((2, reach)),
                dma((3, nx - 1)),
                dma((3, nx - 1)),
                dma((nx - 1,)),
                dma((nx - 1,)),
                dma((groups, nx - 1)),
                dma((groups, nx - 1)),
                dma,
                dma,
                dma((nx, groups)),
                dma((nx - 1, groups)),
            ],
            compiler_params=pltpu.CompilerParams(
                collective_id=0, has_side_effects=True, vmem_limit_bytes=60 * 2**20
            ),
            name="attend",
        )(queries, comp_k, comp_v, prompt_k, prompt_v, output_grad, lengths)

    rows = P(("groups", "prompt"), "sample", "fsdp", None)
    prompt_rows = P(("groups", "prompt"), ("sample", "fsdp"), None)
    return jax.shard_map(
        shards,
        mesh=mesh,
        in_specs=(rows, rows, rows, prompt_rows, prompt_rows, rows, P(("groups", "prompt"), "sample")),
        out_specs=(rows, rows, rows, rows, prompt_rows, prompt_rows),
        check_vma=False,
    )
```

time: 293 us -> 104 us (0.35)
  blocking collectives: 109 us -> 0 us
  Pallas kernels: 0 us -> 96.2 us
  matrix products: 62 us -> 0 us
  waiting for transfers between devices: 39.6 us -> 0 us
  local copies, waits for them, and re-layouts: 45.4 us -> 6.47 us
  between operations: 15.2 us -> 1.3 us
  starting transfers between devices: 12.8 us -> 0 us
  other arithmetic: 7.58 us -> 0 us
    all_gather x2 -> x0, blocking collectives: 109 us -> none  [side_by_side(): lax.all_gather(both, axis, axis=dim, tiled=True)]
    pallas_call x0 -> x1, Pallas kernels: none -> 96.2 us  [shards(): pl.pallas_call(functools.partial(kernel, nz, nx), out_shape=(one(queries....]
    dot_general x24 -> x0, matrix products: 52.4 us -> none  [the longest x4 14.2 us: shards(): jnp.einsum('rtj,jd->trd', attention_half, value_block, preferred_element_...]
    all_to_all x3 -> x0, waiting for transfers between devices: 39.5 us -> none  [the longest x2 36.5 us: sent_and_summed(): lax.all_to_all(in_blocks(value, dim, devices), axis, 0, 0, tiled=True)]
    all_to_all x3 -> x0, starting transfers between devices: 12.7 us -> none  [the longest x2 8.76 us: sent_and_summed(): lax.all_to_all(in_blocks(value, dim, devices), axis, 0, 0, tiled=True)]
    slice x14 -> x0, local copies, waits for them, and re-layouts: 11.5 us -> none  [the longest x5 5.55 us: shards(): gradient_row_slice[:, first_column:first_column + group_width]]
    unnamed x71 -> x16, local copies, waits for them, and re-layouts: 17.9 us -> 6.47 us
    reshape x10 -> x0, local copies, waits for them, and re-layouts: 11.2 us -> none  [the longest x4 4.81 us: shards(): mixed_parts.append(blended_output.reshape(row_count, group_width))]
  transfers between devices with their start and end apart: 4 -> 0, of which waited for: 3 -> 0; matrix products, arithmetic and copies ran while one was open for 11% -> 0% of each run, Pallas kernels for 0% -> 0%
where the time goes in v1:
time: 104 us
  Pallas kernels  96.2 us (92%)
  local copies, waits for them, and re-layouts  6.47 us (6%)
  between operations  1.3 us (1%)
    pallas_call x1, Pallas kernels, shards(): pl.pallas_call(functools.partial(kernel, nz, nx), out_shape=(one(queries....  96.2 us
    unnamed x16, local copies, waits for them, and re-layouts  6.47 us

profile of v1, /device:TPU:40, one launch (start us, length us, event | category | flops | bytes accessed | tf_op | source)
XLA Modules:
  0.0 104.0 jit_solution(12116164531114265461)
XLA Ops:
  1.3 96.2 %attend.1 = (bf16[1,1,128,4096]{3,2,1,0:T(8,128)(2,1)}, bf16[1,1,128,4096]{3,2,1,0:T(8,128)(2,1)}, f32[1,1,128,512]{3,2,1,0:T(8,128)}, f32[1,1,128,512]{3,2,1,0:...) custom-call(bf16[1,1,128,4096]{3,2,1,0:T(8,128)(2,1)} %queries.1, bf16[1,1,128,512]{3,2,1,0:T(8,128)(2,1)} %comp_k.1, ...), custom_call_target="tpu_custom_call" | custom-call | tf_op jit(solution)/shard_map/attend/pallas_call | solution.py:451
  97.5 0.0 copy-start
  97.5 2.4 %copy.20 = bf16[1,1,128,4096]{3,2,1,0:T(8,128)(2,1)} copy(bf16[1,1,128,4096]{3,2,1,0:T(8,128)(2,1)} %get-tuple-element.12) | data formatting | bytes 2097152
  99.9 0.0 copy-done
  99.9 0.0 copy-start.2
  99.9 1.0 copy.21
  100.8 0.1 copy-done.2
  101.0 0.0 copy-start.1
  101.0 0.7 copy.22
  101.7 0.3 copy-done.1
  102.0 0.0 copy-start.4
  102.0 0.7 copy.23
  102.7 0.0 copy-done.4
  102.7 0.0 copy-start.3
  102.7 0.6 copy.24
  103.3 0.1 copy-done.3
  103.4 0.6 copy.25
Async XLA Ops:
  97.5 2.4 %copy-start = (bf16[1,1,128,4096]{3,2,1,0:T(8,128)(2,1)S(1)}, bf16[1,1,128,4096]{3,2,1,0:T(8,128)(2,1)}, u32[]{:S(2)}) copy-start(bf16[1,1,128,4096]{3,2,1,0:T(8,128)(2,1)} %get-tuple-element.13) | copy-start | bytes 3145732
  99.9 1.1 %copy-start.2 = (f32[1,1,128,512]{3,2,1,0:T(8,128)S(1)}, f32[1,1,128,512]{3,2,1,0:T(8,128)}, u32[]{:S(2)}) copy-start(f32[1,1,128,512]{3,2,1,0:T(8,128)} %get-tuple-element.14) | copy-start | bytes 786436
  101.0 1.0 %copy-start.1 = (f32[1,1,128,512]{3,2,1,0:T(8,128)S(1)}, f32[1,1,128,512]{3,2,1,0:T(8,128)}, u32[]{:S(2)}) copy-start(f32[1,1,128,512]{3,2,1,0:T(8,128)} %get-tuple-element.15) | copy-start | bytes 786436
  102.0 0.7 copy-start.4
  102.7 0.7 copy-start.3

commit v2 on v1

--- a/solution.py
+++ b/solution.py
@@ -51,12 +51,11 @@
     blockmax,
     p_half,
     ds_half,
-    o_half,
-    dq_half,
+    pp_s,
+    dsp_s,
     csend,
     crecv,
     cown,
-    cstage,
     xsend,
     xown,
     xrecv,
@@ -66,8 +65,6 @@
     pstage,
     in_sem,
     kvin_sem,
-    out_sem,
-    gout_sem,
     r1_send,
     r1_recv,
     r2_send,
@@ -147,7 +144,7 @@
         keys = kv[b, 0, :, cols]
         values = kv[b, 1, :, cols]
         values_t = kvt[b, 1, cols, :]
-        slot = g * (nx + 1) + b
+        slot = g * nx + b
         for t in range(wide // TILE):
             at = slice(t * TILE, (t + 1) * TILE)
             src = pl.ds(pl.multiple_of(g * wide + t * TILE, TILE), TILE)
@@ -181,7 +178,7 @@
     def backward(b, g, first):
         cols = pl.ds(pl.multiple_of(g * HEAD_DIM, HEAD_DIM), HEAD_DIM)
         keys_t = kvt[b, 0, cols, :]
-        slot = g * (nx + 1) + b
+        slot = g * nx + b
         for t in range(wide // TILE):
             at = slice(t * TILE, (t + 1) * TILE)
             factor = jnp.exp2((blockmax[slot, 0:1, at] - stat[g, 0:1, at]) * fold) * stat[g, 1:2, at]
@@ -191,25 +188,43 @@
             ds_half[:, at] = ds
             dq = dot(keys_t, ds)
             if first:
+                dq += dot(kvt[last, 0, cols, :], dsp_s[g, :, at])
                 dq_s[g, :, at] = dq
             else:
                 dq_s[g, :, at] += dq
         src = pl.ds(pl.multiple_of(g * wide, wide), wide)
         return dot(ds_half[...], q_s[src, :]) * scale, dot(p_half[...], g_s[src, :])
 
-    def flush(source, staged, target, g, sem):
+    def flush(source, target, g):
         for t in range(wide // TILE):
-            at = slice(t * TILE, (t + 1) * TILE)
-            dst = pl.ds(pl.multiple_of(g * wide + t * TILE, TILE), TILE)
-            staged[dst, :] = source(at).T.astype(BF16)
-        for h in range(share):
-            head = g * share + h
-            cols = pl.ds(pl.multiple_of(head * HEAD_DIM, HEAD_DIM), HEAD_DIM)
-            src = pl.ds(pl.multiple_of(head * count, count), count)
-            pltpu.make_async_copy(staged.at[src], target.at[0, 0, :, cols], sem).start()
+            block = source(slice(t * TILE, (t + 1) * TILE)).T.astype(BF16)
+            for h in range(TILE // count):
+                head = g * share + t * (TILE // count) + h
+                cols = pl.ds(pl.multiple_of(head * HEAD_DIM, HEAD_DIM), HEAD_DIM)
+                target[0, 0, :, cols] = block[h * count : (h + 1) * count]
+
+    pl.semaphore_wait(barrier, len(near) + nx - 1)
+
+    first_leg = {
+        d: remote(
+            rows.at[0, 0], rows.at[0, (nz - d) % nz], r1_send.at[n], r1_recv.at[n], at_z(d)
+        )
+        for n, d in enumerate(near)
+    }
+    for d in sorted(near, key=abs, reverse=True):
+        first_leg[d].start()
+
+    def kv_copy(d):
+        return remote(kv.at[x], kv.at[x], kv_send.at[d - 1], kv_recv.at[d - 1], at_x(d))
 
     for c in own_kv:
         c.wait()
+    for d in range(1, nx):
+
+        @pl.when(x + d < nx)
+        def _(d=d):
+            kv_copy(d).start()
+
     turn(x)
     token = lax.broadcasted_iota(jnp.int32, (count, HEAD_DIM), 0) + x * count
     length = jnp.full((count, HEAD_DIM), lengths[0, 0], jnp.int32)
@@ -224,26 +239,6 @@
             at = pl.ds(pl.multiple_of((g * share + h) * count, count), count)
             g_s[at, :] = (g_s[at, :].astype(F32) * weight).astype(BF16)
         forward(x, g, True)
-
-    pl.semaphore_wait(barrier, len(near) + nx - 1)
-
-    first_leg = {
-        d: remote(
-            rows.at[0, 0], rows.at[0, (nz - d) % nz], r1_send.at[n], r1_recv.at[n], at_z(d)
-        )
-        for n, d in enumerate(near)
-    }
-    for d in sorted(near, key=abs, reverse=True):
-        first_leg[d].start()
-
-    def kv_copy(d):
-        return remote(kv.at[x], kv.at[x], kv_send.at[d - 1], kv_recv.at[d - 1], at_x(d))
-
-    for d in range(1, nx):
-
-        @pl.when(x + d < nx)
-        def _(d=d):
-            kv_copy(d).start()
 
     second_leg = []
     for e in range(1, reach + 1):
@@ -292,20 +287,34 @@
         def _(g):
             forward(b, g, False)
 
-    for c in second_leg:
-        c.wait_recv()
-    final_legs = to_columns(2, reach + 1, nz - reach)
-    for c in final_legs:
-        c.start()
-    column_legs += final_legs
+    ahead, behind = second_leg[0::2], second_leg[1::2]
+    ahead += behind[reach - 1 :]
+    behind = behind[: reach - 1]
+    half = reach // 2
+    pieces = [
+        (ahead[:half], reach + 1, reach + 1 + half),
+        (behind[:half], nz - reach - half, nz - reach),
+        (ahead[half:], reach + 1 + half, 2 * reach + 1),
+        (behind[half:], 2 * reach + 1, nz - reach - half),
+    ]
+    for n, (arrivals, begin, end) in enumerate(pieces):
+        for c in arrivals:
+            c.wait_recv()
+        if end > begin:
+            legs = to_columns(2 + n, begin, end)
+            for c in legs:
+                c.start()
+            column_legs += legs
     for c in column_legs:
         c.wait_recv()
 
-    rows32[...] = rows[...].reshape(key_count, 2 * groups, HEAD_DIM).astype(F32)
+    for d in range(nx):
+        part_rows = nz * 2 * groups
+        rows32[d * part_rows : (d + 1) * part_rows, :] = rows[d].astype(F32).reshape(part_rows, HEAD_DIM)
     for part in range(2):
         for g in range(groups):
             cols = slice(g * HEAD_DIM, (g + 1) * HEAD_DIM)
-            block = rows32[:, part * groups + g, :]
+            block = rows32[pl.ds(part * groups + g, key_count, stride=2 * groups), :]
             kv[last, part, :, cols] = block.astype(BF16)
             kvt[last, part, cols, :] = block.T.astype(BF16)
 
@@ -316,28 +325,45 @@
 
     @pl.loop(0, groups)
     def _(g):
-        forward(last, g, False)
-        inverse = 1.0 / stat[g, 1:2, :]
-        stat[g, 1:2, :] = inverse
-        stat[g, 2:3, :] = stat[g, 2:3, :] * inverse
-        both = backward(last, g, True)
+        cols = pl.ds(pl.multiple_of(g * HEAD_DIM, HEAD_DIM), HEAD_DIM)
+        keys = kv[last, 0, :, cols]
+        values = kv[last, 1, :, cols]
+        for t in range(wide // TILE):
+            at = slice(t * TILE, (t + 1) * TILE)
+            src = pl.ds(pl.multiple_of(g * wide + t * TILE, TILE), TILE)
+            s = dot(keys, q_s[src, :], NT)
+            before = stat[g, 0:1, at]
+            top = jnp.maximum(jnp.max(s, axis=0, keepdims=True), before)
+            e = jnp.exp2((s - top) * fold)
+            old = jnp.exp2((before - top) * fold)
+            inverse = 1.0 / (old * stat[g, 1:2, at] + jnp.sum(e, axis=0, keepdims=True))
+            dp = dot(values, g_s[src, :], NT)
+            p = e * inverse
+            mean = old * inverse * stat[g, 2:3, at] + jnp.sum(p * dp, axis=0, keepdims=True)
+            pp_s[g, :, at] = p.astype(BF16)
+            dsp_s[g, :, at] = (p * (dp - mean)).astype(BF16)
+            stat[g, 0:1, at] = top
+            stat[g, 1:2, at] = inverse
+            stat[g, 2:3, at] = mean
+            stat[g, 3:4, at] = old * inverse
+        src = pl.ds(pl.multiple_of(g * wide, wide), wide)
+        both = dot(dsp_s[g], q_s[src, :]) * scale, dot(pp_s[g], g_s[src, :])
         for part in range(2):
             xown[g, part] = both[part][:nz]
             for d in range(1, nx):
                 xsend[g, d, part] = both[part][d * nz : (d + 1) * nz].astype(BF16)
         for d in range(1, nx):
             x_copy(g, d).start()
-        flush(lambda at: o_s[g, :, at] * stat[g, 1:2, at], o_half, out, g, out_sem.at[0])
 
     def c_copy(b, g, d):
         return remote(
             csend.at[b, g], crecv.at[d - 1, g], c_send.at[b, g], c_recv.at[d - 1, g], {"fsdp": b}
         )
 
-    def completion_backward(b):
+    def completion_backward(b, first):
         @pl.loop(0, groups)
         def _(g):
-            both = backward(b, g, False)
+            both = backward(b, g, first)
 
             @pl.when(b < x)
             def _():
@@ -350,7 +376,7 @@
                 for part in range(2):
                     cown[g, part] = both[part]
 
-    completion_backward(0)
+    completion_backward(0, True)
 
     for g in range(groups):
         for d in range(1, nx):
@@ -360,8 +386,8 @@
             total = xown[g, part]
             for d in range(1, nx):
                 total += xrecv[g, d, part].astype(F32)
-            zf[:, part * groups + g, :] = total
-    zsend[...] = zf[...].astype(BF16)
+            zf[pl.ds(part * groups + g, nz, stride=2 * groups), :] = total
+    zsend[...] = zf[...].reshape(nz, 2 * groups, HEAD_DIM).astype(BF16)
 
     def z_copy(s):
         return remote(zsend.at[s], zrecv.at[nz - s], z_send, z_recv, at_z(s))
@@ -371,11 +397,21 @@
 
     @pl.loop(1, x + 1)
     def _(b):
-        completion_backward(b)
+        completion_backward(b, False)
 
     @pl.loop(0, groups)
     def _(g):
-        flush(lambda at: dq_s[g, :, at] * scale, dq_half, query_grad, g, out_sem.at[1])
+        cols = pl.ds(pl.multiple_of(g * HEAD_DIM, HEAD_DIM), HEAD_DIM)
+        values_t = kvt[last, 1, cols, :]
+        flush(
+            lambda at: o_s[g, :, at] * stat[g, 3:4, at] + dot(values_t, pp_s[g, :, at]),
+            out,
+            g,
+        )
+
+    @pl.loop(0, groups)
+    def _(g):
+        flush(lambda at: dq_s[g, :, at] * scale, query_grad, g)
 
     for d in range(1, nx):
 
@@ -388,23 +424,9 @@
                 for part in range(2):
                     cown[g, part] += crecv[d - 1, g, part].astype(F32)
 
-    for part in range(2):
+    for part, ref in enumerate((comp_k_grad, comp_v_grad)):
         for g in range(groups):
-            cstage[part, :, g * HEAD_DIM : (g + 1) * HEAD_DIM] = cown[g, part]
-    grads_out = [
-        pltpu.make_async_copy(cstage.at[0], comp_k_grad.at[0, 0], gout_sem.at[0]),
-        pltpu.make_async_copy(cstage.at[1], comp_v_grad.at[0, 0], gout_sem.at[1]),
-    ]
-    for c in grads_out:
-        c.start()
-
-    pltpu.make_async_copy(zrecv.at[1:nz], zrecv.at[1:nz], z_recv).wait()
-    total = zf[0]
-    for s in range(1, nz):
-        total += zrecv[s].astype(F32)
-    for k, ref in enumerate((prompt_k_grad, prompt_v_grad)):
-        for g in range(groups):
-            ref[0, :, g * HEAD_DIM : (g + 1) * HEAD_DIM] = total[k * groups + g : k * groups + g + 1, :]
+            ref[0, 0, :, g * HEAD_DIM : (g + 1) * HEAD_DIM] = cown[g, part]
 
     for c in list(first_leg.values()) + second_leg + column_legs:
         c.wait_send()
@@ -425,9 +447,22 @@
                 csend.at[b, g], crecv.at[0, g], c_send.at[b, g], c_recv.at[0, g], at_x(1)
             ).wait_send()
 
-    pltpu.make_async_copy(o_half, o_half, out_sem.at[0]).wait()
-    pltpu.make_async_copy(dq_half, dq_half, out_sem.at[1]).wait()
-    for c in grads_out:
+    pltpu.make_async_copy(zrecv.at[1:nz], zrecv.at[1:nz], z_recv).wait()
+    total = zf[: 2 * groups, :]
+    for s in range(1, nz):
+        total += zrecv[s].astype(F32)
+    for k, ref in enumerate((prompt_k_grad, prompt_v_grad)):
+        for g in range(groups):
+            ref[0, :, g * HEAD_DIM : (g + 1) * HEAD_DIM] = total[k * groups + g : k * groups + g + 1, :]
+
+
+def hand_on(*refs):
+    n = len(refs) // 2
+    sem = refs[-1]
+    copies = [pltpu.make_async_copy(refs[k], refs[n + k], sem.at[k]) for k in range(n)]
+    for c in copies:
+        c.start()
+    for c in copies:
         c.wait()
 
 
@@ -448,56 +483,53 @@
         smem = pl.BlockSpec(memory_space=pltpu.SMEM)
         dma = pltpu.SemaphoreType.DMA
         one = jax.ShapeDtypeStruct
-        return pl.pallas_call(
+        results = pl.pallas_call(
             functools.partial(kernel, nz, nx),
             out_shape=(
-                one(queries.shape, BF16),
-                one(queries.shape, BF16),
-                one(comp_k.shape, F32),
-                one(comp_k.shape, F32),
-                one(prompt_k.shape, F32),
-                one(prompt_k.shape, F32),
+                pltpu.VMEM(queries.shape, BF16),
+                pltpu.VMEM(queries.shape, BF16),
+                pltpu.VMEM(comp_k.shape, F32),
+                pltpu.VMEM(comp_k.shape, F32),
+                pltpu.VMEM(prompt_k.shape, F32),
+                pltpu.VMEM(prompt_k.shape, F32),
             ),
             in_specs=[anywhere, anywhere, anywhere, vmem, vmem, anywhere, smem],
-            out_specs=(anywhere, anywhere, anywhere, anywhere, vmem, vmem),
+            out_specs=(vmem,) * 6,
             scratch_shapes=[
                 pltpu.VMEM((heads * count, HEAD_DIM), BF16),
                 pltpu.VMEM((heads * count, HEAD_DIM), BF16),
                 pltpu.VMEM((blocks, 2, count, kv_width), BF16),
                 pltpu.VMEM((blocks, 2, kv_width, count), BF16),
                 pltpu.VMEM((nx, nz, 2 * groups, HEAD_DIM), BF16),
-                pltpu.VMEM((key_count, 2 * groups, HEAD_DIM), F32),
-                pltpu.VMEM((groups * blocks, count, wide), F32),
-                pltpu.VMEM((groups * blocks, count, wide), F32),
+                pltpu.VMEM((key_count * 2 * groups, HEAD_DIM), F32),
+                pltpu.VMEM((groups * nx, count, wide), F32),
+                pltpu.VMEM((groups * nx, count, wide), F32),
                 pltpu.VMEM((groups, HEAD_DIM, wide), F32),
                 pltpu.VMEM((groups, HEAD_DIM, wide), F32),
                 pltpu.VMEM((groups, 8, wide), F32),
-                pltpu.VMEM((groups * blocks, 1, wide), F32),
+                pltpu.VMEM((groups * nx, 1, wide), F32),
                 pltpu.VMEM((count, wide), BF16),
                 pltpu.VMEM((count, wide), BF16),
-                pltpu.VMEM((heads * count, HEAD_DIM), BF16),
-                pltpu.VMEM((heads * count, HEAD_DIM), BF16),
+                pltpu.VMEM((groups, key_count, wide), BF16),
+                pltpu.VMEM((groups, key_count, wide), BF16),
                 pltpu.VMEM((nx, groups, 2, count, HEAD_DIM), BF16),
                 pltpu.VMEM((nx - 1, groups, 2, count, HEAD_DIM), BF16),
                 pltpu.VMEM((groups, 2, count, HEAD_DIM), F32),
-                pltpu.VMEM((2, count, kv_width), F32),
                 pltpu.VMEM((groups, nx, 2, nz, HEAD_DIM), BF16),
                 pltpu.VMEM((groups, 2, nz, HEAD_DIM), F32),
                 pltpu.VMEM((groups, nx, 2, nz, HEAD_DIM), BF16),
-                pltpu.VMEM((nz, 2 * groups, HEAD_DIM), F32),
+                pltpu.VMEM((nz * 2 * groups, HEAD_DIM), F32),
                 pltpu.VMEM((nz, 2 * groups, HEAD_DIM), BF16),
                 pltpu.VMEM((nz, 2 * groups, HEAD_DIM), BF16),
                 pltpu.VMEM((2 * groups, HEAD_DIM), F32),
                 dma((2, groups)),
                 dma((2,)),
-                dma((2,)),
-                dma((2,)),
                 dma((2 * reach,)),
                 dma((2 * reach,)),
                 dma((2, reach)),
                 dma((2, reach)),
-                dma((3, nx - 1)),
-                dma((3, nx - 1)),
+                dma((6, nx - 1)),
+                dma((6, nx - 1)),
                 dma((nx - 1,)),
                 dma((nx - 1,)),
                 dma((groups, nx - 1)),
@@ -508,10 +540,20 @@
                 dma((nx - 1, groups)),
             ],
             compiler_params=pltpu.CompilerParams(
-                collective_id=0, has_side_effects=True, vmem_limit_bytes=60 * 2**20
+                collective_id=0, has_side_effects=True, vmem_limit_bytes=58 * 2**20
             ),
             name="attend",
         )(queries, comp_k, comp_v, prompt_k, prompt_v, output_grad, lengths)
+        n = len(results)
+        return pl.pallas_call(
+            hand_on,
+            out_shape=tuple(one(r.shape, r.dtype) for r in results),
+            in_specs=[vmem] * n,
+            out_specs=(anywhere,) * n,
+            scratch_shapes=[dma((n,))],
+            compiler_params=pltpu.CompilerParams(vmem_limit_bytes=2**20),
+            name="hand_on",
+        )(*(pltpu.with_memory_space_constraint(r, pltpu.VMEM) for r in results))
 
     rows = P(("groups", "prompt"), "sample", "fsdp", None)
     prompt_rows = P(("groups", "prompt"), ("sample", "fsdp"), None)

time: 104 us -> 96.4 us (0.927)
  local copies, waits for them, and re-layouts: 6.47 us -> 0 us
  Pallas kernels: 96.2 us -> 95 us
    unnamed x16 -> x0, local copies, waits for them, and re-layouts: 6.47 us -> none
    pallas_call x1 -> x2, Pallas kernels: 96.2 us -> 95 us  [the longest x1 93.4 us: shards(): pl.pallas_call(functools.partial(kernel, nz, nx), out_shape=(pltpu.VMEM(q...]
where the time goes in v2:
time: 96.4 us; the launch traced here: 96.3 us
  Pallas kernels  95 us (99%)
  between operations  1.29 us (1%)
    pallas_call x1, Pallas kernels, shards(): pl.pallas_call(functools.partial(kernel, nz, nx), out_shape=(pltpu.VMEM(q...  93.4 us

profile of v2, /device:TPU:40, one launch (start us, length us, event | category | flops | bytes accessed | tf_op | source)
XLA Modules:
  0.0 96.3 jit_solution(445276508149559624)
XLA Ops:
  1.3 93.4 %attend.1 = (bf16[1,1,128,4096]{3,2,1,0:T(8,128)(2,1)S(1)}, bf16[1,1,128,4096]{3,2,1,0:T(8,128)(2,1)S(1)}, f32[1,1,128,512]{3,2,1,0:T(8,128)S(1)}, f32[1,1,128,5...) custom-call(bf16[1,1,128,4096]{3,2,1,0:T(8,128)(2,1)} %queries.1, ...), custom_call_target="tpu_custom_call" | custom-call | tf_op jit(solution)/shard_map/attend/pallas_call | solution.py:486
  94.7 1.5 %hand_on.1 = (bf16[1,1,128,4096]{3,2,1,0:T(8,128)(2,1)}, bf16[1,1,128,4096]{3,2,1,0:T(8,128)(2,1)}, f32[1,1,128,512]{3,2,1,0:T(8,128)}, f32[1,1,128,512]{3,2,1,0...) custom-call(bf16[1,1,128,4096]{3,2,1,0:T(8,128)(2,1)S(1)} %get-tuple-element.12.refs_0_, ...), custom_call_target="tpu_custom_call" | custom-call | tf_op jit(solution)/shard_map/hand_on/pallas_call | solution.py:548

commit v3 on v2

--- a/solution.py
+++ b/solution.py
@@ -13,12 +13,10 @@
 MESH = pl.DeviceIdType.MESH
 F32 = jnp.float32
 BF16 = jnp.bfloat16
-NT = (((1,), (1,)), ((), ()))
-NN = (((1,), (0,)), ((), ()))
-
-
-def dot(a, b, dims=NN):
-    return lax.dot_general(a, b, dims, preferred_element_type=F32)
+
+
+def dot(a, b):
+    return jnp.dot(a, b, preferred_element_type=F32)
 
 
 def kernel(
@@ -39,6 +37,8 @@
     prompt_v_grad,
     q_s,
     g_s,
+    qt_s,
+    gt_s,
     kv,
     kvt,
     rows,
@@ -63,8 +63,10 @@
     zsend,
     zrecv,
     pstage,
+    pin,
     in_sem,
     kvin_sem,
+    pin_sem,
     r1_send,
     r1_recv,
     r2_send,
@@ -87,6 +89,7 @@
     heads = queries.shape[3] // HEAD_DIM
     share = heads // groups
     wide = share * count
+    tiles = wide // TILE
     reach = nz // 4
     scale = HEAD_DIM**-0.5
     fold = scale * math.log2(math.e)
@@ -104,11 +107,22 @@
             src_ref=src, dst_ref=dst, send_sem=send, recv_sem=recv, device_id=to, device_id_type=MESH
         )
 
+    barrier = pltpu.get_barrier_semaphore()
+    near = [d for d in range(1, reach + 1)] + [-d for d in range(1, reach + 1)]
+    for d in near:
+        pl.semaphore_signal(barrier, inc=1, device_id=at_z(d), device_id_type=MESH)
+    for d in range(1, nx):
+        pl.semaphore_signal(barrier, inc=1, device_id=at_x(d), device_id_type=MESH)
+
     own_kv = [
         pltpu.make_async_copy(comp_k.at[0, 0], kv.at[x, 0], kvin_sem.at[0]),
         pltpu.make_async_copy(comp_v.at[0, 0], kv.at[x, 1], kvin_sem.at[1]),
     ]
-    for c in own_kv:
+    own_rows = [
+        pltpu.make_async_copy(prompt_k, pin.at[0], pin_sem.at[0]),
+        pltpu.make_async_copy(prompt_v, pin.at[1], pin_sem.at[1]),
+    ]
+    for c in own_rows + own_kv:
         c.start()
 
     @pl.loop(0, groups)
@@ -120,22 +134,16 @@
             pltpu.make_async_copy(queries.at[0, 0, :, cols], q_s.at[dst], in_sem.at[0, g]).start()
             pltpu.make_async_copy(out_grad.at[0, 0, :, cols], g_s.at[dst], in_sem.at[1, g]).start()
 
-    for k, ref in enumerate((prompt_k, prompt_v)):
-        row = ref[0].astype(F32)
+    for k in range(2):
+        own_rows[k].wait()
+        row = pin[k, 0].astype(F32)
         for g in range(groups):
             pstage[k * groups + g : k * groups + g + 1, :] = row[:, g * HEAD_DIM : (g + 1) * HEAD_DIM]
     rows[0, 0] = pstage[...].astype(BF16)
 
-    barrier = pltpu.get_barrier_semaphore()
-    near = [d for d in range(1, reach + 1)] + [-d for d in range(1, reach + 1)]
-    for d in near:
-        pl.semaphore_signal(barrier, inc=1, device_id=at_z(d), device_id_type=MESH)
-    for d in range(1, nx):
-        pl.semaphore_signal(barrier, inc=1, device_id=at_x(d), device_id_type=MESH)
-
-    def turn(b):
+    def turn(b, begin, end):
         for part in range(2):
-            for g in range(groups):
+            for g in range(begin, end):
                 cols = slice(g * HEAD_DIM, (g + 1) * HEAD_DIM)
                 kvt[b, part, cols, :] = kv[b, part, :, cols].astype(F32).T.astype(BF16)
 
@@ -145,10 +153,9 @@
         values = kv[b, 1, :, cols]
         values_t = kvt[b, 1, cols, :]
         slot = g * nx + b
-        for t in range(wide // TILE):
+        for t in range(tiles):
             at = slice(t * TILE, (t + 1) * TILE)
-            src = pl.ds(pl.multiple_of(g * wide + t * TILE, TILE), TILE)
-            s = dot(keys, q_s[src, :], NT)
+            s = dot(keys, qt_s[g * tiles + t])
             if first:
                 key = lax.broadcasted_iota(jnp.int32, s.shape, 0)
                 token = lax.broadcasted_iota(jnp.int32, s.shape, 1) % count
@@ -159,7 +166,7 @@
                 top = jnp.maximum(top, before)
             e = jnp.exp2((s - top) * fold)
             total = jnp.sum(e, axis=0, keepdims=True)
-            dp = dot(values, g_s[src, :], NT)
+            dp = dot(values, gt_s[g * tiles + t])
             mean = jnp.sum(e * dp, axis=0, keepdims=True)
             o = dot(values_t, e.astype(BF16))
             if not first:
@@ -179,7 +186,7 @@
         cols = pl.ds(pl.multiple_of(g * HEAD_DIM, HEAD_DIM), HEAD_DIM)
         keys_t = kvt[b, 0, cols, :]
         slot = g * nx + b
-        for t in range(wide // TILE):
+        for t in range(tiles):
             at = slice(t * TILE, (t + 1) * TILE)
             factor = jnp.exp2((blockmax[slot, 0:1, at] - stat[g, 0:1, at]) * fold) * stat[g, 1:2, at]
             p = e_s[slot, :, at] * factor
@@ -196,7 +203,7 @@
         return dot(ds_half[...], q_s[src, :]) * scale, dot(p_half[...], g_s[src, :])
 
     def flush(source, target, g):
-        for t in range(wide // TILE):
+        for t in range(tiles):
             block = source(slice(t * TILE, (t + 1) * TILE)).T.astype(BF16)
             for h in range(TILE // count):
                 head = g * share + t * (TILE // count) + h
@@ -214,18 +221,23 @@
     for d in sorted(near, key=abs, reverse=True):
         first_leg[d].start()
 
-    def kv_copy(d):
-        return remote(kv.at[x], kv.at[x], kv_send.at[d - 1], kv_recv.at[d - 1], at_x(d))
+    middle = groups // 2
+
+    def kv_copy(half, d, b):
+        cols = pl.ds(half * middle * HEAD_DIM, middle * HEAD_DIM)
+        block = kv.at[b, :, :, cols]
+        return remote(block, block, kv_send.at[half, d - 1], kv_recv.at[half, d - 1], at_x(d))
 
     for c in own_kv:
         c.wait()
-    for d in range(1, nx):
-
-        @pl.when(x + d < nx)
-        def _(d=d):
-            kv_copy(d).start()
-
-    turn(x)
+    for half in range(2):
+        for d in range(1, nx):
+
+            @pl.when(x + d < nx)
+            def _(half=half, d=d):
+                kv_copy(half, d, x).start()
+
+    turn(x, 0, groups)
     token = lax.broadcasted_iota(jnp.int32, (count, HEAD_DIM), 0) + x * count
     length = jnp.full((count, HEAD_DIM), lengths[0, 0], jnp.int32)
     weight = jnp.where(token < length, F32(count * nx) / length.astype(F32), 0.0)
@@ -238,6 +250,10 @@
         for h in range(share):
             at = pl.ds(pl.multiple_of((g * share + h) * count, count), count)
             g_s[at, :] = (g_s[at, :].astype(F32) * weight).astype(BF16)
+        for t in range(tiles):
+            src = pl.ds(pl.multiple_of(g * wide + t * TILE, TILE), TILE)
+            qt_s[g * tiles + t] = q_s[src, :].astype(F32).T.astype(BF16)
+            gt_s[g * tiles + t] = g_s[src, :].astype(F32).T.astype(BF16)
         forward(x, g, True)
 
     second_leg = []
@@ -276,16 +292,26 @@
     for c in column_legs:
         c.start()
 
-    @pl.loop(0, x)
-    def _(n):
-        d = n + 1
-        b = x - d
-        remote(kv.at[b], kv.at[b], kv_send.at[n], kv_recv.at[n], at_x(1)).wait_recv()
-        turn(b)
-
-        @pl.loop(0, groups)
-        def _(g):
-            forward(b, g, False)
+    def earlier(half):
+        @pl.loop(0, nx - 1)
+        def _(n):
+            d = lax.rem(n + nx - 2, nx - 1) + 1
+
+            @pl.when(d <= x)
+            def _():
+                b = x - d
+                cols = pl.ds(half * middle * HEAD_DIM, middle * HEAD_DIM)
+                block = kv.at[b, :, :, cols]
+                remote(
+                    block, block, kv_send.at[half, d - 1], kv_recv.at[half, d - 1], at_x(1)
+                ).wait_recv()
+                turn(b, half * middle, (half + 1) * middle)
+
+                @pl.loop(half * middle, (half + 1) * middle)
+                def _(g):
+                    forward(b, g, False)
+
+    earlier(0)
 
     ahead, behind = second_leg[0::2], second_leg[1::2]
     ahead += behind[reach - 1 :]
@@ -305,6 +331,9 @@
             for c in legs:
                 c.start()
             column_legs += legs
+
+    earlier(1)
+
     for c in column_legs:
         c.wait_recv()
 
@@ -328,16 +357,15 @@
         cols = pl.ds(pl.multiple_of(g * HEAD_DIM, HEAD_DIM), HEAD_DIM)
         keys = kv[last, 0, :, cols]
         values = kv[last, 1, :, cols]
-        for t in range(wide // TILE):
+        for t in range(tiles):
             at = slice(t * TILE, (t + 1) * TILE)
-            src = pl.ds(pl.multiple_of(g * wide + t * TILE, TILE), TILE)
-            s = dot(keys, q_s[src, :], NT)
+            s = dot(keys, qt_s[g * tiles + t])
             before = stat[g, 0:1, at]
             top = jnp.maximum(jnp.max(s, axis=0, keepdims=True), before)
             e = jnp.exp2((s - top) * fold)
             old = jnp.exp2((before - top) * fold)
             inverse = 1.0 / (old * stat[g, 1:2, at] + jnp.sum(e, axis=0, keepdims=True))
-            dp = dot(values, g_s[src, :], NT)
+            dp = dot(values, gt_s[g * tiles + t])
             p = e * inverse
             mean = old * inverse * stat[g, 2:3, at] + jnp.sum(p * dp, axis=0, keepdims=True)
             pp_s[g, :, at] = p.astype(BF16)
@@ -376,7 +404,7 @@
                 for part in range(2):
                     cown[g, part] = both[part]
 
-    completion_backward(0, True)
+    completion_backward(x, True)
 
     for g in range(groups):
         for d in range(1, nx):
@@ -395,7 +423,7 @@
     for s in sorted(range(1, nz), key=lambda s: min(s, nz - s), reverse=True):
         z_copy(s).start()
 
-    @pl.loop(1, x + 1)
+    @pl.loop(0, x)
     def _(b):
         completion_backward(b, False)
 
@@ -434,7 +462,8 @@
 
         @pl.when(x + d < nx)
         def _(d=d):
-            kv_copy(d).wait_send()
+            for half in range(2):
+                kv_copy(half, d, x).wait_send()
 
         for g in range(groups):
             x_copy(g, d).wait_send()
@@ -493,11 +522,13 @@
                 pltpu.VMEM(prompt_k.shape, F32),
                 pltpu.VMEM(prompt_k.shape, F32),
             ),
-            in_specs=[anywhere, anywhere, anywhere, vmem, vmem, anywhere, smem],
+            in_specs=[anywhere] * 6 + [smem],
             out_specs=(vmem,) * 6,
             scratch_shapes=[
                 pltpu.VMEM((heads * count, HEAD_DIM), BF16),
                 pltpu.VMEM((heads * count, HEAD_DIM), BF16),
+                pltpu.VMEM((heads * count // TILE, HEAD_DIM, TILE), BF16),
+                pltpu.VMEM((heads * count // TILE, HEAD_DIM, TILE), BF16),
                 pltpu.VMEM((blocks, 2, count, kv_width), BF16),
                 pltpu.VMEM((blocks, 2, kv_width, count), BF16),
                 pltpu.VMEM((nx, nz, 2 * groups, HEAD_DIM), BF16),
@@ -522,7 +553,9 @@
                 pltpu.VMEM((nz, 2 * groups, HEAD_DIM), BF16),
                 pltpu.VMEM((nz, 2 * groups, HEAD_DIM), BF16),
                 pltpu.VMEM((2 * groups, HEAD_DIM), F32),
+                pltpu.VMEM((2, *prompt_k.shape), BF16),
                 dma((2, groups)),
+                dma((2,)),
                 dma((2,)),
                 dma((2 * reach,)),
                 dma((2 * reach,)),
@@ -530,8 +563,8 @@
                 dma((2, reach)),
                 dma((6, nx - 1)),
                 dma((6, nx - 1)),
-                dma((nx - 1,)),
-                dma((nx - 1,)),
+                dma((2, nx - 1)),
+                dma((2, nx - 1)),
                 dma((groups, nx - 1)),
                 dma((groups, nx - 1)),
                 dma,

time: 96.4 us -> 90.8 us (0.942)
  Pallas kernels: 95 us -> 89.3 us
    pallas_call x1, Pallas kernels: 93.4 us -> 87.8 us  [shards(): pl.pallas_call(functools.partial(kernel, nz, nx), out_shape=(pltpu.VMEM(q...]
where the time goes in v3:
time: 90.8 us; the launch traced here: 90.6 us
  Pallas kernels  89.3 us (98%)
  between operations  1.29 us (1%)
    pallas_call x1, Pallas kernels, shards(): pl.pallas_call(functools.partial(kernel, nz, nx), out_shape=(pltpu.VMEM(q...  87.8 us

profile of v3, /device:TPU:40, one launch (start us, length us, event | category | flops | bytes accessed | tf_op | source)
XLA Modules:
  0.0 90.6 jit_solution(12864264307840898427)
XLA Ops:
  1.3 87.8 %attend.1 = (bf16[1,1,128,4096]{3,2,1,0:T(8,128)(2,1)S(1)}, bf16[1,1,128,4096]{3,2,1,0:T(8,128)(2,1)S(1)}, f32[1,1,128,512]{3,2,1,0:T(8,128)S(1)}, f32[1,1,128,5...) custom-call(bf16[1,1,128,4096]{3,2,1,0:T(8,128)(2,1)} %queries.1, ...), custom_call_target="tpu_custom_call" | custom-call | tf_op jit(solution)/shard_map/attend/pallas_call | solution.py:515
  89.1 1.5 %hand_on.1 = (bf16[1,1,128,4096]{3,2,1,0:T(8,128)(2,1)}, bf16[1,1,128,4096]{3,2,1,0:T(8,128)(2,1)}, f32[1,1,128,512]{3,2,1,0:T(8,128)}, f32[1,1,128,512]{3,2,1,0...) custom-call(bf16[1,1,128,4096]{3,2,1,0:T(8,128)(2,1)S(1)} %get-tuple-element.12.refs_0_, ...), custom_call_target="tpu_custom_call" | custom-call | tf_op jit(solution)/shard_map/hand_on/pallas_call | solution.py:581

commit v4 on v3

--- a/solution.py
+++ b/solution.py
@@ -56,6 +56,7 @@
     csend,
     crecv,
     cown,
+    cterm,
     xsend,
     xown,
     xrecv,
@@ -223,26 +224,43 @@
 
     middle = groups // 2
 
-    def kv_copy(half, d, b):
+    def kv_copy(half, b, kind, to):
         cols = pl.ds(half * middle * HEAD_DIM, middle * HEAD_DIM)
         block = kv.at[b, :, :, cols]
-        return remote(block, block, kv_send.at[half, d - 1], kv_recv.at[half, d - 1], at_x(d))
+        return remote(block, block, kv_send.at[half, kind], kv_recv.at[half, b], {"fsdp": to})
+
+    own_sends = [(p, half, p, 0, p + 1) for half in range(2) for p in range(nx - 1)]
+    own_sends += [(0, half, 0, 1, nx - 1) for half in range(2)] + [(1, 1, 1, 1, 0)]
+    pass_first = [(1, 0, 0, 2, 2), (2, 0, 1, 2, 3)]
+    pass_second = [(1, 1, 0, 2, 2), (0, 1, 1, 2, 3)]
+
+    def own_send(entry):
+        p, half, b, kind, to = entry
+
+        @pl.when(x == p)
+        def _():
+            kv_copy(half, b, kind, to).start()
+
+    def pass_on(entry):
+        p, half, b, kind, to = entry
+
+        @pl.when(x == p)
+        def _():
+            c = kv_copy(half, b, kind, to)
+            c.wait_recv()
+            c.start()
 
     for c in own_kv:
         c.wait()
-    for half in range(2):
-        for d in range(1, nx):
-
-            @pl.when(x + d < nx)
-            def _(half=half, d=d):
-                kv_copy(half, d, x).start()
+    for entry in own_sends:
+        own_send(entry)
 
     turn(x, 0, groups)
     token = lax.broadcasted_iota(jnp.int32, (count, HEAD_DIM), 0) + x * count
     length = jnp.full((count, HEAD_DIM), lengths[0, 0], jnp.int32)
     weight = jnp.where(token < length, F32(count * nx) / length.astype(F32), 0.0)
 
-    @pl.loop(0, groups)
+    @pl.loop(0, groups, unroll=2)
     def _(g):
         src = pl.ds(pl.multiple_of(g * wide, wide), wide)
         pltpu.make_async_copy(q_s.at[src], q_s.at[src], in_sem.at[0, g]).wait()
@@ -255,6 +273,9 @@
             qt_s[g * tiles + t] = q_s[src, :].astype(F32).T.astype(BF16)
             gt_s[g * tiles + t] = g_s[src, :].astype(F32).T.astype(BF16)
         forward(x, g, True)
+
+    for entry in pass_first:
+        pass_on(entry)
 
     second_leg = []
     for e in range(1, reach + 1):
@@ -300,16 +321,20 @@
             @pl.when(d <= x)
             def _():
                 b = x - d
-                cols = pl.ds(half * middle * HEAD_DIM, middle * HEAD_DIM)
-                block = kv.at[b, :, :, cols]
-                remote(
-                    block, block, kv_send.at[half, d - 1], kv_recv.at[half, d - 1], at_x(1)
-                ).wait_recv()
+                passed = (x == 1) if half else (x == 1) | ((x == 2) & (b == 1))
+
+                @pl.when(jnp.logical_not(passed))
+                def _():
+                    kv_copy(half, b, 0, lax.rem(x + 1, nx)).wait_recv()
+
                 turn(b, half * middle, (half + 1) * middle)
 
-                @pl.loop(half * middle, (half + 1) * middle)
+                @pl.loop(half * middle, (half + 1) * middle, unroll=2)
                 def _(g):
                     forward(b, g, False)
+
+    for entry in pass_second:
+        pass_on(entry)
 
     earlier(0)
 
@@ -352,7 +377,7 @@
             xsend.at[g, d], xrecv.at[g, nx - d], x_send.at[g, d - 1], x_recv.at[g, d - 1], at_x(d)
         )
 
-    @pl.loop(0, groups)
+    @pl.loop(0, groups, unroll=2)
     def _(g):
         cols = pl.ds(pl.multiple_of(g * HEAD_DIM, HEAD_DIM), HEAD_DIM)
         keys = kv[last, 0, :, cols]
@@ -383,28 +408,41 @@
         for d in range(1, nx):
             x_copy(g, d).start()
 
-    def c_copy(b, g, d):
-        return remote(
-            csend.at[b, g], crecv.at[d - 1, g], c_send.at[b, g], c_recv.at[d - 1, g], {"fsdp": b}
-        )
-
-    def completion_backward(b, first):
-        @pl.loop(0, groups)
-        def _(g):
-            both = backward(b, g, first)
-
-            @pl.when(b < x)
-            def _():
+    def c_copy(b, g, slot, to):
+        return remote(csend.at[b, g], crecv.at[slot, g], c_send.at[b, g], c_recv.at[slot, g], {"fsdp": to})
+
+    @pl.loop(0, groups, unroll=2)
+    def _(g):
+        both = backward(x, g, True)
+        for part in range(2):
+            cown[g, part] = both[part]
+
+    def earlier_backward(n):
+        edge = x == nx - 1
+        b = lax.rem(n + edge.astype(jnp.int32), nx - 1)
+        short = edge & (b == 0)
+        more = jnp.logical_not(edge) & ((b > 0) | (x < nx - 2))
+        slot = jnp.where(short, nx - 1, b)
+        to = jnp.where(short, 0, x - 1)
+
+        @pl.loop(0, groups // 2)
+        def _(pair):
+            for k in range(2):
+                both = backward(b, 2 * pair + k, False)
                 for part in range(2):
-                    csend[b, g, part] = both[part].astype(BF16)
-                c_copy(b, g, x - b).start()
-
-            @pl.when(b == x)
-            def _():
+                    cterm[k, part] = both[part]
+            for k in range(2):
+                g = 2 * pair + k
+
+                @pl.when(more)
+                def _(g=g, k=k):
+                    c_copy(b, g, b, to).wait_recv()
+                    for part in range(2):
+                        cterm[k, part] += crecv[b, g, part].astype(F32)
+
                 for part in range(2):
-                    cown[g, part] = both[part]
-
-    completion_backward(x, True)
+                    csend[b, g, part] = cterm[k, part].astype(BF16)
+                c_copy(b, g, slot, to).start()
 
     for g in range(groups):
         for d in range(1, nx):
@@ -423,9 +461,9 @@
     for s in sorted(range(1, nz), key=lambda s: min(s, nz - s), reverse=True):
         z_copy(s).start()
 
-    @pl.loop(0, x)
-    def _(b):
-        completion_backward(b, False)
+    @pl.loop(0, jnp.minimum(x, 1))
+    def _(n):
+        earlier_backward(n)
 
     @pl.loop(0, groups)
     def _(g):
@@ -437,34 +475,42 @@
             g,
         )
 
+    @pl.loop(1, x)
+    def _(n):
+        earlier_backward(n)
+
     @pl.loop(0, groups)
     def _(g):
         flush(lambda at: dq_s[g, :, at] * scale, query_grad, g)
 
-    for d in range(1, nx):
-
-        @pl.when(x + d < nx)
-        def _(d=d):
-            for g in range(groups):
-                remote(
-                    csend.at[0, g], crecv.at[d - 1, g], c_send.at[0, g], c_recv.at[d - 1, g], at_x(d)
-                ).wait_recv()
-                for part in range(2):
-                    cown[g, part] += crecv[d - 1, g, part].astype(F32)
+    def collect(slot):
+        for g in range(groups):
+            c_copy(0, g, slot, lax.rem(x + 1, nx)).wait_recv()
+            for part in range(2):
+                cown[g, part] += crecv[slot, g, part].astype(F32)
+
+    @pl.when((x < nx - 1) & ((x > 0) | (x < nx - 2)))
+    def _():
+        collect(x)
+
+    @pl.when(x == 0)
+    def _():
+        collect(nx - 1)
 
     for part, ref in enumerate((comp_k_grad, comp_v_grad)):
         for g in range(groups):
             ref[0, 0, :, g * HEAD_DIM : (g + 1) * HEAD_DIM] = cown[g, part]
 
+    for entry in own_sends + pass_first + pass_second:
+
+        @pl.when(x == entry[0])
+        def _(entry=entry):
+            kv_copy(*entry[1:]).wait_send()
+
     for c in list(first_leg.values()) + second_leg + column_legs:
         c.wait_send()
     for d in range(1, nx):
 
-        @pl.when(x + d < nx)
-        def _(d=d):
-            for half in range(2):
-                kv_copy(half, d, x).wait_send()
-
         for g in range(groups):
             x_copy(g, d).wait_send()
     pltpu.make_async_copy(zsend.at[1:nz], zsend.at[1:nz], z_send).wait()
@@ -472,9 +518,7 @@
     @pl.loop(0, x)
     def _(b):
         for g in range(groups):
-            remote(
-                csend.at[b, g], crecv.at[0, g], c_send.at[b, g], c_recv.at[0, g], at_x(1)
-            ).wait_send()
+            c_copy(b, g, 0, lax.rem(x + 1, nx)).wait_send()
 
     pltpu.make_async_copy(zrecv.at[1:nz], zrecv.at[1:nz], z_recv).wait()
     total = zf[: 2 * groups, :]
@@ -544,8 +588,9 @@
                 pltpu.VMEM((groups, key_count, wide), BF16),
                 pltpu.VMEM((groups, key_count, wide), BF16),
                 pltpu.VMEM((nx, groups, 2, count, HEAD_DIM), BF16),
-                pltpu.VMEM((nx - 1, groups, 2, count, HEAD_DIM), BF16),
+                pltpu.VMEM((nx, groups, 2, count, HEAD_DIM), BF16),
                 pltpu.VMEM((groups, 2, count, HEAD_DIM), F32),
+                pltpu.VMEM((2, 2, count, HEAD_DIM), F32),
                 pltpu.VMEM((groups, nx, 2, nz, HEAD_DIM), BF16),
                 pltpu.VMEM((groups, 2, nz, HEAD_DIM), F32),
                 pltpu.VMEM((groups, nx, 2, nz, HEAD_DIM), BF16),
@@ -563,14 +608,14 @@
                 dma((2, reach)),
                 dma((6, nx - 1)),
                 dma((6, nx - 1)),
-                dma((2, nx - 1)),
-                dma((2, nx - 1)),
+                dma((2, 3)),
+                dma((2, nx)),
                 dma((groups, nx - 1)),
                 dma((groups, nx - 1)),
                 dma,
                 dma,
                 dma((nx, groups)),
-                dma((nx - 1, groups)),
+                dma((nx, groups)),
             ],
             compiler_params=pltpu.CompilerParams(
                 collective_id=0, has_side_effects=True, vmem_limit_bytes=58 * 2**20

time: 90.8 us -> 88.3 us (0.972)
  Pallas kernels: 89.3 us -> 86.7 us
    pallas_call x1, Pallas kernels: 87.8 us -> 85.2 us  [shards(): pl.pallas_call(functools.partial(kernel, nz, nx), out_shape=(pltpu.VMEM(q...]
where the time goes in v4:
time: 88.3 us; the launch traced here: 88 us
  Pallas kernels  86.7 us (98%)
  between operations  1.29 us (1%)
    pallas_call x1, Pallas kernels, shards(): pl.pallas_call(functools.partial(kernel, nz, nx), out_shape=(pltpu.VMEM(q...  85.2 us

profile of v4, /device:TPU:40, one launch (start us, length us, event | category | flops | bytes accessed | tf_op | source)
XLA Modules:
  0.0 88.0 jit_solution(15143157307932399869)
XLA Ops:
  1.3 85.2 %attend.1 = (bf16[1,1,128,4096]{3,2,1,0:T(8,128)(2,1)S(1)}, bf16[1,1,128,4096]{3,2,1,0:T(8,128)(2,1)S(1)}, f32[1,1,128,512]{3,2,1,0:T(8,128)S(1)}, f32[1,1,128,5...) custom-call(bf16[1,1,128,4096]{3,2,1,0:T(8,128)(2,1)} %queries.1, ...), custom_call_target="tpu_custom_call" | custom-call | tf_op jit(solution)/shard_map/attend/pallas_call | solution.py:559
  86.5 1.5 %hand_on.1 = (bf16[1,1,128,4096]{3,2,1,0:T(8,128)(2,1)}, bf16[1,1,128,4096]{3,2,1,0:T(8,128)(2,1)}, f32[1,1,128,512]{3,2,1,0:T(8,128)}, f32[1,1,128,512]{3,2,1,0...) custom-call(bf16[1,1,128,4096]{3,2,1,0:T(8,128)(2,1)S(1)} %get-tuple-element.12.refs_0_, ...), custom_call_target="tpu_custom_call" | custom-call | tf_op jit(solution)/shard_map/hand_on/pallas_call | solution.py:626

commit v5 on v4

--- a/solution.py
+++ b/solution.py
@@ -215,7 +215,7 @@
 
     first_leg = {
         d: remote(
-            rows.at[0, 0], rows.at[0, (nz - d) % nz], r1_send.at[n], r1_recv.at[n], at_z(d)
+            rows.at[0, 0], rows.at[0, (nz - d) % nz], r1_send, r1_recv.at[n], at_z(d)
         )
         for n, d in enumerate(near)
     }
@@ -281,7 +281,7 @@
     for e in range(1, reach + 1):
         first_leg[-e].wait_recv()
         c = remote(
-            rows.at[0, e], rows.at[0, reach + e], r2_send.at[0, e - 1], r2_recv.at[0, e - 1], at_z(-reach)
+            rows.at[0, e], rows.at[0, reach + e], r2_send, r2_recv.at[0, e - 1], at_z(-reach)
         )
         c.start()
         second_leg.append(c)
@@ -290,26 +290,26 @@
             c = remote(
                 rows.at[0, nz - e],
                 rows.at[0, nz - reach - e],
-                r2_send.at[1, e - 1],
+                r2_send,
                 r2_recv.at[1, e - 1],
                 at_z(reach),
             )
             c.start()
             second_leg.append(c)
 
-    def to_columns(part, begin, end):
+    def to_columns(begin, end):
         return [
             remote(
                 rows.at[0, begin:end],
                 rows.at[nx - d, begin:end],
-                rx_send.at[part, d - 1],
-                rx_recv.at[part, d - 1],
+                rx_send,
+                rx_recv,
                 at_x(d),
             )
             for d in range(1, nx)
         ]
 
-    column_legs = to_columns(0, 0, reach + 1) + to_columns(1, nz - reach, nz)
+    column_legs = to_columns(0, reach + 1) + to_columns(nz - reach, nz)
     for c in column_legs:
         c.start()
 
@@ -348,19 +348,16 @@
         (ahead[half:], reach + 1 + half, 2 * reach + 1),
         (behind[half:], 2 * reach + 1, nz - reach - half),
     ]
-    for n, (arrivals, begin, end) in enumerate(pieces):
+    for arrivals, begin, end in pieces:
         for c in arrivals:
             c.wait_recv()
         if end > begin:
-            legs = to_columns(2 + n, begin, end)
-            for c in legs:
+            for c in to_columns(begin, end):
                 c.start()
-            column_legs += legs
 
     earlier(1)
 
-    for c in column_legs:
-        c.wait_recv()
+    pltpu.make_async_copy(rows.at[1:nx], rows.at[1:nx], rx_recv).wait()
 
     for d in range(nx):
         part_rows = nz * 2 * groups
@@ -374,10 +371,10 @@
 
     def x_copy(g, d):
         return remote(
-            xsend.at[g, d], xrecv.at[g, nx - d], x_send.at[g, d - 1], x_recv.at[g, d - 1], at_x(d)
+            xsend.at[g, d], xrecv.at[g, nx - d], x_send, x_recv, at_x(d)
         )
 
-    @pl.loop(0, groups, unroll=2)
+    @pl.loop(0, groups, unroll=groups)
     def _(g):
         cols = pl.ds(pl.multiple_of(g * HEAD_DIM, HEAD_DIM), HEAD_DIM)
         keys = kv[last, 0, :, cols]
@@ -444,9 +441,7 @@
                     csend[b, g, part] = cterm[k, part].astype(BF16)
                 c_copy(b, g, slot, to).start()
 
-    for g in range(groups):
-        for d in range(1, nx):
-            x_copy(g, d).wait_recv()
+    pltpu.make_async_copy(xrecv.at[:, 1:nx], xrecv.at[:, 1:nx], x_recv).wait()
     for g in range(groups):
         for part in range(2):
             total = xown[g, part]
@@ -507,12 +502,12 @@
         def _(entry=entry):
             kv_copy(*entry[1:]).wait_send()
 
-    for c in list(first_leg.values()) + second_leg + column_legs:
-        c.wait_send()
-    for d in range(1, nx):
-
-        for g in range(groups):
-            x_copy(g, d).wait_send()
+    sent = rows.at[0, 0 : 2 * reach]
+    pltpu.make_async_copy(sent, sent, r1_send).wait()
+    sent = rows.at[0, 0 : 2 * reach - 1]
+    pltpu.make_async_copy(sent, sent, r2_send).wait()
+    pltpu.make_async_copy(rows.at[1:nx], rows.at[1:nx], rx_send).wait()
+    pltpu.make_async_copy(xsend.at[:, 1:nx], xsend.at[:, 1:nx], x_send).wait()
     pltpu.make_async_copy(zsend.at[1:nz], zsend.at[1:nz], z_send).wait()
 
     @pl.loop(0, x)
@@ -602,16 +597,16 @@
                 dma((2, groups)),
                 dma((2,)),
                 dma((2,)),
+                dma,
                 dma((2 * reach,)),
-                dma((2 * reach,)),
+                dma,
                 dma((2, reach)),
-                dma((2, reach)),
-                dma((6, nx - 1)),
-                dma((6, nx - 1)),
+                dma,
+                dma,
                 dma((2, 3)),
                 dma((2, nx)),
-                dma((groups, nx - 1)),
-                dma((groups, nx - 1)),
+                dma,
+                dma,
                 dma,
                 dma,
                 dma((nx, groups)),

time: 88.3 us -> 87.1 us (0.986)
  Pallas kernels: 86.7 us -> 85.7 us
    pallas_call x1, Pallas kernels: 85.2 us -> 84.2 us  [shards(): pl.pallas_call(functools.partial(kernel, nz, nx), out_shape=(pltpu.VMEM(q...]
where the time goes in v5:
time: 87.1 us; the launch traced here: 87 us
  Pallas kernels  85.7 us (98%)
  between operations  1.29 us (1%)
    pallas_call x1, Pallas kernels, shards(): pl.pallas_call(functools.partial(kernel, nz, nx), out_shape=(pltpu.VMEM(q...  84.2 us

profile of v5, /device:TPU:40, one launch (start us, length us, event | category | flops | bytes accessed | tf_op | source)
XLA Modules:
  0.0 87.0 jit_solution(14713287154067447942)
XLA Ops:
  1.3 84.2 %attend.1 = (bf16[1,1,128,4096]{3,2,1,0:T(8,128)(2,1)S(1)}, bf16[1,1,128,4096]{3,2,1,0:T(8,128)(2,1)S(1)}, f32[1,1,128,512]{3,2,1,0:T(8,128)S(1)}, f32[1,1,128,5...) custom-call(bf16[1,1,128,4096]{3,2,1,0:T(8,128)(2,1)} %queries.1, ...), custom_call_target="tpu_custom_call" | custom-call | tf_op jit(solution)/shard_map/attend/pallas_call | solution.py:554
  85.4 1.5 %hand_on.1 = (bf16[1,1,128,4096]{3,2,1,0:T(8,128)(2,1)}, bf16[1,1,128,4096]{3,2,1,0:T(8,128)(2,1)}, f32[1,1,128,512]{3,2,1,0:T(8,128)}, f32[1,1,128,512]{3,2,1,0...) custom-call(bf16[1,1,128,4096]{3,2,1,0:T(8,128)(2,1)S(1)} %get-tuple-element.12.refs_0_, ...), custom_call_target="tpu_custom_call" | custom-call | tf_op jit(solution)/shard_map/hand_on/pallas_call | solution.py:621

commit v6 on v5

--- a/solution.py
+++ b/solution.py
@@ -408,7 +408,7 @@
     def c_copy(b, g, slot, to):
         return remote(csend.at[b, g], crecv.at[slot, g], c_send.at[b, g], c_recv.at[slot, g], {"fsdp": to})
 
-    @pl.loop(0, groups, unroll=2)
+    @pl.loop(0, groups, unroll=groups)
     def _(g):
         both = backward(x, g, True)
         for part in range(2):

time: 87.1 us -> 87.1 us (level)
  no operation moved by 1% of the time
where the time goes in v6:
time: 87.1 us; the launch traced here: 87 us
  Pallas kernels  85.7 us (98%)
  between operations  1.29 us (1%)
    pallas_call x1, Pallas kernels, shards(): pl.pallas_call(functools.partial(kernel, nz, nx), out_shape=(pltpu.VMEM(q...  84.2 us

profile of v6, /device:TPU:40, one launch (start us, length us, event | category | flops | bytes accessed | tf_op | source)
XLA Modules:
  0.0 87.0 jit_solution(12707621019812623888)
XLA Ops:
  1.3 84.2 %attend.1 = (bf16[1,1,128,4096]{3,2,1,0:T(8,128)(2,1)S(1)}, bf16[1,1,128,4096]{3,2,1,0:T(8,128)(2,1)S(1)}, f32[1,1,128,512]{3,2,1,0:T(8,128)S(1)}, f32[1,1,128,5...) custom-call(bf16[1,1,128,4096]{3,2,1,0:T(8,128)(2,1)} %queries.1, ...), custom_call_target="tpu_custom_call" | custom-call | tf_op jit(solution)/shard_map/attend/pallas_call | solution.py:554
  85.4 1.5 %hand_on.1 = (bf16[1,1,128,4096]{3,2,1,0:T(8,128)(2,1)}, bf16[1,1,128,4096]{3,2,1,0:T(8,128)(2,1)}, f32[1,1,128,512]{3,2,1,0:T(8,128)}, f32[1,1,128,512]{3,2,1,0...) custom-call(bf16[1,1,128,4096]{3,2,1,0:T(8,128)(2,1)S(1)} %get-tuple-element.12.refs_0_, ...), custom_call_target="tpu_custom_call" | custom-call | tf_op jit(solution)/shard_map/hand_on/pallas_call | solution.py:621
